TPU v7x, 256 devices: a whole 4x4x8 slice. The times are simulated.
256 devices in a mesh: section: 4 (over y), dp: 64 (over x, z, core).
Axes of the slice: x: 4, y: 4, z: 8, core: 2. Of those that a mesh axis runs over, the one named last changes fastest.
Arguments:
- token_ids: int32 [4, 4096], P(None, 'dp'), may hold values from 0 to 127
- embed: bfloat16 [128, 512], replicated, may hold values from -6 to 6
- weights: bfloat16 [4, 2, 512, 2048], P('section'), may hold values from -0.25 to 0.25
- variance: bfloat16 [4, 1024, 2048], P('section', 'dp'), may hold values from 9.9658966e-05 to 0.0099487305
- momentum: bfloat16 [4, 1024, 2048], P('section', 'dp'), may hold values from -4 to 4
- worker_error: bfloat16 [4, 64, 2, 512, 2048], P('section', 'dp'), may hold values from -6 to 6
- server_error: float32 [4, 1024, 2048], P('section', 'dp'), may hold values from -0.75 to 0.75
- cotangent: bfloat16 [4, 4096, 512], P(None, 'dp'), may hold values from -0.75 to 0.75
Outputs:
- new_weights: bfloat16 [4, 1024, 2048], P('section', 'dp')
- new_momentum: bfloat16 [4, 1024, 2048], P('section', 'dp')
- new_worker_error: bfloat16 [4, 64, 2, 512, 2048], P('section', 'dp')
- new_server_error: float32 [4, 1024, 2048], P('section', 'dp')
All inputs are finite; a program needn't handle non-finite values.
Results may differ from a plain program's by a relative error of at most 0.012.
Values may be sent and summed in bfloat16 or wider, within the bound.
A program may use at most 128 MiB of HBM per device.

v0:
```python
import math

import jax
import jax.numpy as jnp
from jax import lax
from jax.sharding import PartitionSpec as P

gelu_coef = math.sqrt(2.0 / math.pi)


def passed_along(array, axis, by):
    count = lax.axis_size(axis)
    pairs = [(i, i + by) for i in range(count) if 0 <= i + by < count]
    return lax.ppermute(array, axis, pairs)


def gelu_value(upper):
    inner = gelu_coef * (upper + 0.044715 * upper * upper * upper)
    return 0.5 * upper * (1.0 + jnp.tanh(inner))


def gelu_slope(upper):
    inner = gelu_coef * (upper + 0.044715 * upper * upper * upper)
    bent = jnp.tanh(inner)
    return 0.5 * (1.0 + bent) + 0.5 * upper * (1.0 - bent * bent) * gelu_coef * (
        1.0 + 3.0 * 0.044715 * upper * upper
    )


def normalize(inputs):
    values = inputs.astype(jnp.float32)
    center = jnp.mean(values, axis=-1, keepdims=True)
    spread = jnp.mean((values - center) * (values - center), axis=-1, keepdims=True)
    scaled = lax.rsqrt(spread + 1e-05)
    return ((values - center) * scaled, scaled)


def forward_block(inputs, first_matrix, second_matrix):
    normed, scaled = normalize(inputs)
    normed_b = normed.astype(jnp.bfloat16)
    upper = jnp.dot(normed_b, first_matrix, preferred_element_type=jnp.float32)
    hidden = gelu_value(upper).astype(jnp.bfloat16)
    mixed = lax.dot_general(
        hidden, second_matrix, (((1,), (1,)), ((), ())), preferred_element_type=jnp.float32
    )
    output = (inputs.astype(jnp.float32) + mixed).astype(jnp.bfloat16)
    return (output, normed, scaled, normed_b, upper, hidden)


def backward_block(grad_out, normed, scaled, upper, first_matrix, second_matrix):
    back_hidden = jnp.dot(grad_out, second_matrix, preferred_element_type=jnp.float32)
    back_upper = (back_hidden * gelu_slope(upper)).astype(jnp.bfloat16)
    back_normed = lax.dot_general(
        back_upper, first_matrix, (((1,), (1,)), ((), ())), preferred_element_type=jnp.float32
    )
    first_mean = jnp.mean(back_normed, axis=-1, keepdims=True)
    second_mean = jnp.mean(back_normed * normed, axis=-1, keepdims=True)
    grad_in = (
        grad_out.astype(jnp.float32) + scaled * (back_normed - first_mean - normed * second_mean)
    ).astype(jnp.bfloat16)
    return (grad_in, back_upper)


def row_product(left, right):
    return lax.dot_general(
        left, right, (((0,), (0,)), ((), ())), preferred_element_type=jnp.float32
    )


def local(token_ids, embed, weights, variance, momentum, worker_error, server_error, cotangent):
    section_count = lax.axis_size("section")
    section_index = lax.axis_index("section")
    replicas = lax.axis_size("dp")
    micro = token_ids.shape[0]
    rows = token_ids.shape[1]
    vocab = embed.shape[0]
    width = embed.shape[1]
    channels = weights.shape[3]
    owned = 2 * width // replicas
    shared = lax.all_gather(momentum[0], "dp", axis=0, tiled=True)
    first_matrix = weights[0, 0]
    second_matrix = weights[0, 1]
    one_hot = (token_ids[:, :, None] == lax.broadcasted_iota(jnp.int32, (1, 1, vocab), 2)).astype(
        jnp.bfloat16
    )
    embedded = jnp.einsum("mtv,vd->mtd", one_hot, embed, preferred_element_type=jnp.float32).astype(
        jnp.bfloat16
    )
    steps = micro + section_count - 1
    incoming = jnp.zeros((rows, width), jnp.bfloat16)
    saved_normed, saved_scaled, saved_bf, saved_upper, saved_hidden = ([], [], [], [], [])
    for step in range(steps):
        index = jnp.clip(step - section_index, 0, micro - 1)
        fresh = lax.dynamic_index_in_dim(embedded, index, 0, keepdims=False)
        inputs = jnp.where(section_index == 0, fresh, incoming)
        output, normed, scaled, normed_b, upper, hidden = forward_block(
            inputs, first_matrix, second_matrix
        )
        saved_normed.append(normed)
        saved_scaled.append(scaled)
        saved_bf.append(normed_b)
        saved_upper.append(upper)
        saved_hidden.append(hidden)
        if step + 1 < steps:
            incoming = passed_along(output, "section", 1)
    normed_all = jnp.stack(saved_normed)
    scaled_all = jnp.stack(saved_scaled)
    normed_bf_all = jnp.stack(saved_bf)
    upper_all = jnp.stack(saved_upper)
    hidden_all = jnp.stack(saved_hidden)
    grad_first = jnp.zeros((width, channels), jnp.float32)
    grad_second = jnp.zeros((width, channels), jnp.float32)
    back_in = jnp.zeros((rows, width), jnp.bfloat16)
    for step in range(steps):
        micro_index = step - (section_count - 1 - section_index)
        valid = jnp.logical_and(micro_index >= 0, micro_index < micro)
        clipped = jnp.clip(micro_index, 0, micro - 1)
        slot = jnp.clip(micro_index + section_index, 0, steps - 1)
        arriving = lax.dynamic_index_in_dim(cotangent, clipped, 0, keepdims=False)
        grad_out = jnp.where(section_index == section_count - 1, arriving, back_in)
        normed = lax.dynamic_index_in_dim(normed_all, slot, 0, keepdims=False)
        scaled = lax.dynamic_index_in_dim(scaled_all, slot, 0, keepdims=False)
        normed_b = lax.dynamic_index_in_dim(normed_bf_all, slot, 0, keepdims=False)
        upper = lax.dynamic_index_in_dim(upper_all, slot, 0, keepdims=False)
        hidden = lax.dynamic_index_in_dim(hidden_all, slot, 0, keepdims=False)
        grad_in, back_upper = backward_block(
            grad_out, normed, scaled, upper, first_matrix, second_matrix
        )
        grad_first = grad_first + jnp.where(valid, row_product(normed_b, back_upper), 0.0)
        grad_second = grad_second + jnp.where(valid, row_product(grad_out, hidden), 0.0)
        if step + 1 < steps:
            back_in = passed_along(grad_in, "section", -1)
    gradient = jnp.stack([grad_first, grad_second])
    combined = (
        0.9 * shared.astype(jnp.float32).reshape(2, width, channels)
        + 0.1 * gradient
        + worker_error[0, 0].astype(jnp.float32)
    )
    worker_scale = jnp.sqrt(jnp.mean(combined * combined) + 0.01)
    packed = (worker_scale * jnp.tanh(combined / worker_scale)).astype(jnp.bfloat16)
    new_worker = (combined - packed.astype(jnp.float32)).astype(jnp.bfloat16)[None, None]
    flat = packed.reshape(2 * width, channels)
    received = lax.all_to_all(
        flat.reshape(replicas, owned, channels), "dp", split_axis=0, concat_axis=0, tiled=True
    )
    total = jnp.sum(received.astype(jnp.float32), axis=0)
    merged = total / replicas + server_error[0]
    server_scale = jnp.sqrt(jnp.mean(merged * merged) + 0.01)
    server_values = (server_scale * jnp.tanh(merged / server_scale)).astype(jnp.bfloat16)
    new_server = (merged - server_values.astype(jnp.float32))[None]
    start = lax.axis_index("dp") * owned
    own_weights = lax.dynamic_slice_in_dim(weights[0].reshape(2 * width, channels), start, owned, 0)
    step_size = (
        0.01
        * server_values.astype(jnp.float32)
        / (jnp.sqrt(variance[0].astype(jnp.float32)) + 1e-08)
    )
    new_weights = (own_weights.astype(jnp.float32) - step_size).astype(jnp.bfloat16)[None]
    return (new_weights, server_values[None], new_worker, new_server)


def solution(mesh):
    in_specs = (
        P(None, "dp"),
        P(),
        P("section", None, None, None),
        P("section", "dp", None),
        P("section", "dp", None),
        P("section", "dp", None, None, None),
        P("section", "dp", None),
        P(None, "dp", None),
    )
    out_specs = (
        P("section", "dp", None),
        P("section", "dp", None),
        P("section", "dp", None, None, None),
        P("section", "dp", None),
    )
    return jax.shard_map(local, mesh=mesh, in_specs=in_specs, out_specs=out_specs, check_vma=False)
```

profile of v0, /device:TPU:1, one launch (start us, length us, event | category | flops | bytes accessed | tf_op | source)
XLA Modules:
  0.0 287.5 jit_solution(2251841772525739811)
XLA Ops:
  9.4 2.9 %bitcast_dynamic-update-slice_fusion.6 = (f32[7,64,2048]{2,1,0:T(8,128)}, f32[64,2048]{1,0:T(8,128)S(1)}) fusion(bf16[1,2,512,2048]{3,2,1,0:T(8,128)(2,1)} %param.10, f32[64]{0:T(128)S(1)} %add_rsqrt_fusion.6, f32[64]{0:T(128)S(1)} %broadcast_multiply_fusion.18, bf16[4,64,512]{2,1,0:T(8,128)(2,1)S(1)} %convolution_convert_fusion, s32[]{:T(128)S(6)} %min.64, ...), kind=kOutput, calls=%fused_computation.206 | convolution fusion | flops 134381568 | bytes 3212293 | tf_op jit(solution)/shard_map/dot_general | solution.py:41
  12.3 2.4 fusion.89
  14.6 4.0 %collective-permute-start = (bf16[64,512]{1,0:T(8,128)(2,1)S(1)}, bf16[64,512]{1,0:T(8,128)(2,1)S(1)}, u32[]{:S(2)}, u32[]{:S(2)}) collective-permute-start(bf16[64,512]{1,0:T(8,128)(2,1)S(1)} %fusion.89), channel_id=1, source_target_pairs={{0,64},{64,128},{128,192},{1,65},{65,129},{129,193},{2,66},{66,130... | collective-permute-start | bytes 196616 | tf_op jit(solution)/shard_map/ppermute | solution.py:14
  20.4 3.1 %bitcast_dynamic-update-slice_fusion.5 = (f32[7,64,2048]{2,1,0:T(8,128)}, f32[64,2048]{1,0:T(8,128)S(1)}) fusion(f32[7,64,2048]{2,1,0:T(8,128)} %get-tuple-element.36, bf16[1,2,512,2048]{3,2,1,0:T(8,128)(2,1)} %param.10, bf16[64,512]{1,0:T(8,128)(2,1)S(1)} %get-tuple-element.29, f32[64]{0:T(128)S(1)} %add_rsqrt_fusion.5, f32[64]{0:T(128)S(1)} %broadcast_multiply_fusion.17), kind=kOutput, calls=%fused_computation.205 | convolution fusion | flops 134348800 | bytes 3211776 | tf_op jit(solution)/shard_map/dot_general | solution.py:41
  23.5 2.3 fusion.86
  25.8 3.7 %collective-permute-start.1 = (bf16[64,512]{1,0:T(8,128)(2,1)S(1)}, bf16[64,512]{1,0:T(8,128)(2,1)S(1)}, u32[]{:S(2)}, u32[]{:S(2)}) collective-permute-start(bf16[64,512]{1,0:T(8,128)(2,1)S(1)} %fusion.86), channel_id=1, source_target_pairs={{0,64},{64,128},{128,192},{1,65},{65,129},{129,193},{2,66},{66,130... | collective-permute-start | bytes 196616 | tf_op jit(solution)/shard_map/ppermute | solution.py:14
  33.4 3.8 %collective-permute-start.2 = (bf16[64,512]{1,0:T(8,128)(2,1)S(1)}, bf16[64,512]{1,0:T(8,128)(2,1)S(1)}, u32[]{:S(2)}, u32[]{:S(2)}) collective-permute-start(bf16[64,512]{1,0:T(8,128)(2,1)S(1)} %fusion.83), channel_id=1, source_target_pairs={{0,64},{64,128},{128,192},{1,65},{65,129},{129,193},{2,66},{66,130... | collective-permute-start | bytes 196616 | tf_op jit(solution)/shard_map/ppermute | solution.py:14
  40.2 4.1 %collective-permute-start.3 = (bf16[64,512]{1,0:T(8,128)(2,1)S(1)}, bf16[64,512]{1,0:T(8,128)(2,1)S(1)}, u32[]{:S(2)}, u32[]{:S(2)}) collective-permute-start(bf16[64,512]{1,0:T(8,128)(2,1)S(1)} %fusion.80), channel_id=1, source_target_pairs={{0,64},{64,128},{128,192},{1,65},{65,129},{129,193},{2,66},{66,130... | collective-permute-start | bytes 196616 | tf_op jit(solution)/shard_map/ppermute | solution.py:14
  47.4 3.7 %collective-permute-start.4 = (bf16[64,512]{1,0:T(8,128)(2,1)S(1)}, bf16[64,512]{1,0:T(8,128)(2,1)S(1)}, u32[]{:S(2)}, u32[]{:S(2)}) collective-permute-start(bf16[64,512]{1,0:T(8,128)(2,1)S(1)} %fusion.77), channel_id=1, source_target_pairs={{0,64},{64,128},{128,192},{1,65},{65,129},{129,193},{2,66},{66,130... | collective-permute-start | bytes 196616 | tf_op jit(solution)/shard_map/ppermute | solution.py:14
  54.4 4.1 %collective-permute-start.5 = (bf16[64,512]{1,0:T(8,128)(2,1)S(1)}, bf16[64,512]{1,0:T(8,128)(2,1)S(1)}, u32[]{:S(2)}, u32[]{:S(2)}) collective-permute-start(bf16[64,512]{1,0:T(8,128)(2,1)S(1)} %fusion.74), channel_id=1, source_target_pairs={{0,64},{64,128},{128,192},{1,65},{65,129},{129,193},{2,66},{66,130... | collective-permute-start | bytes 196616 | tf_op jit(solution)/shard_map/ppermute | solution.py:14
  61.6 2.7 fusion.300
  67.7 3.4 %collective-permute-done.6 = bf16[64,512]{1,0:T(8,128)(2,1)S(1)} collective-permute-done((bf16[64,512]{1,0:T(8,128)(2,1)S(1)}, bf16[64,512]{1,0:T(8,128)(2,1)S(1)}, u32[]{:S(2)}, u32[]{:S(2)}) %collective-permute-start.6) | collective-permute-done | bytes 65568 | tf_op jit(solution)/shard_map/ppermute | solution.py:14
  71.8 2.7 fusion.296
  77.5 3.4 %collective-permute-done.7 = bf16[64,512]{1,0:T(8,128)(2,1)S(1)} collective-permute-done((bf16[64,512]{1,0:T(8,128)(2,1)S(1)}, bf16[64,512]{1,0:T(8,128)(2,1)S(1)}, u32[]{:S(2)}, u32[]{:S(2)}) %collective-permute-start.7) | collective-permute-done | bytes 65568 | tf_op jit(solution)/shard_map/ppermute | solution.py:14
  81.6 2.7 fusion.294
  87.3 3.0 %collective-permute-done.8 = bf16[64,512]{1,0:T(8,128)(2,1)S(1)} collective-permute-done((bf16[64,512]{1,0:T(8,128)(2,1)S(1)}, bf16[64,512]{1,0:T(8,128)(2,1)S(1)}, u32[]{:S(2)}, u32[]{:S(2)}) %collective-permute-start.8) | collective-permute-done | bytes 65568 | tf_op jit(solution)/shard_map/ppermute | solution.py:14
  93.4 2.7 fusion.292
  100.6 2.7 fusion.290
  106.3 1.5 collective-permute-start.11
  107.8 2.8 fusion.288
  111.7 4.2 %select_add_fusion = f32[512,2048]{1,0:T(8,128)} fusion(f32[512,2048]{1,0:T(8,128)S(1)} %fusion.188, f32[512,2048]{1,0:T(8,128)S(1)} %fusion.190, f32[512,2048]{1,0:T(8,128)S(1)} %fusion.192, f32[512,2048]{1,0:T(8,128)S(1)} %fusion.194, f32[512,2048]{1,0:T(8,128)S(1)} %fusion.196, f32[512,2048]{1,0:T(8,128)S(1)} %fusion.198, pred[]{:T(512)S(6)} %and.29, ...), kind=kOutput, calls=%fused_computation.13 | convolution fusion | flops 147881984 | bytes 29753360 | tf_op jit(solution)/shard_map/dot_general | solution.py:65
  115.9 9.9 %select_add_fusion.1 = f32[512,2048]{1,0:T(8,128)} fusion(f32[512,2048]{1,0:T(8,128)} %fusion.288, f32[512,2048]{1,0:T(8,128)} %fusion.290, f32[512,2048]{1,0:T(8,128)} %fusion.292, f32[512,2048]{1,0:T(8,128)} %fusion.294, f32[512,2048]{1,0:T(8,128)} %fusion.296, f32[512,2048]{1,0:T(8,128)} %fusion.300, pred[]{:T(512)S(6)} %and.29, pred[]{:T(512)S(6)} %and.28, ...), kind=kOutput, calls=%fused_computation.14 | convolution fusion | flops 284590080 | bytes 32183808 | tf_op jit(solution)/shard_map/dot_general | solution.py:65
  125.8 8.5 %maximum_multiply_fusion = f32[2,512,2048]{2,1,0:T(8,128)} fusion(f32[1,512,2048]{2,1,0:T(8,128)} %bitcast.534, f32[1,512,2048]{2,1,0:T(8,128)} %bitcast.536), kind=kLoop, calls=%fused_computation | loop fusion | flops 4194304 | bytes 16777216 | tf_op jit(solution)/shard_map/mul | solution.py:136
  134.3 7.6 %fusion.3 = f32[]{:T(128)} fusion(f32[2,512,2048]{2,1,0:T(8,128)} %maximum_multiply_fusion, bf16[1,1,2,512,2048]{4,3,2,1,0:T(8,128)(2,1)} %param.13, bf16[1,1024,2048]{2,1,0:T(8,128)(2,1)} %all-gather.3.cloned.1.call-done), kind=kLoop, calls=%fused_computation.6 | loop fusion | flops 14680063 | bytes 16777220 | tf_op jit(solution)/shard_map/reduce_sum | solution.py:139
  142.6 3.5 %convert_multiply_fusion = f32[1,1024,2048]{2,1,0:T(8,128)S(1)} fusion(bf16[1,1024,2048]{2,1,0:T(8,128)(2,1)} %all-gather.3.cloned.1.call-done), kind=kLoop, calls=%fused_computation.8 | loop fusion | flops 4194304 | bytes 12582912 | tf_op jit(solution)/shard_map/mul | solution.py:135
  146.1 4.2 %copy-done.3 = f32[1,1024,2048]{2,1,0:T(8,128)} copy-done((f32[1,1024,2048]{2,1,0:T(8,128)}, f32[1,1024,2048]{2,1,0:T(8,128)S(1)}, u32[]{:S(2)}) %copy-start.3) | copy-done | bytes 8388632
  151.4 3.8 %multiply_convert_fusion.1 = bf16[64,16,2048]{2,1,0:T(8,128)(2,1)} fusion(f32[64,16,2048]{2,1,0:T(8,128)S(1)} %bitcast.530, f32[64,16,2048]{2,1,0:T(8,128)S(1)} %bitcast.529, f32[]{:T(128)S(6)} %sqrt.10, bf16[64,16,2048]{2,1,0:T(8,128)(2,1)S(1)} %bitcast.533), kind=kLoop, calls=%fused_computation.12 | loop fusion | flops 12582912 | bytes 25165828 | tf_op jit(solution)/shard_map/convert_element_type | solution.py:140
  155.2 23.1 %all-to-all-start = ((bf16[64,16,2048]{2,1,0:T(8,128)(2,1)}), bf16[64,16,2048]{2,1,0:T(8,128)(2,1)}, u32[]{:S(2)}, u32[]{:S(2)}) async-start(bf16[64,16,2048]{2,1,0:T(8,128)(2,1)} %multiply_convert_fusion.1), calls=%async_computation | async-start | bytes 8388608 | tf_op jit(solution)/shard_map/all_to_all | solution.py:143
  178.3 10.5 %subtract_convert_fusion = bf16[1,1,2,512,2048]{4,3,2,1,0:T(8,128)(2,1)} fusion(f32[1,1,2,512,2048]{4,3,2,1,0:T(8,128)} %bitcast.531, f32[1,1,1,512,2048]{4,3,2,1,0:T(8,128)} %bitcast.535, f32[1,1,1,512,2048]{4,3,2,1,0:T(8,128)} %bitcast.537, f32[]{:T(128)S(6)} %sqrt.10, bf16[1,1,2,512,2048]{4,3,2,1,0:T(8,128)(2,1)} %param.13), kind=kLoop, calls=%fused_computation.9 | loop fusion | flops 23068672 | bytes 25165828 | tf_op jit(solution)/shard_map/convert_element_type | solution.py:141
  188.9 85.3 %all-to-all-done = bf16[64,16,2048]{2,1,0:T(8,128)(2,1)} async-done(((bf16[64,16,2048]{2,1,0:T(8,128)(2,1)}), bf16[64,16,2048]{2,1,0:T(8,128)(2,1)}, u32[]{:S(2)}, u32[]{:S(2)}) %all-to-all-start) | async-done | bytes 4194336 | tf_op jit(solution)/shard_map/all_to_all | solution.py:143
  274.2 2.9 convert_reduce_fusion
  279.1 1.6 fusion.311
  (155 shorter events, 44.4 us)
Async XLA Ops:
  7.2 0.9 copy-start
  7.2 127.1 %all-gather.3.cloned.1.call-start = ((), (), s32[]{:S(2)}) async-start(), calls=%async_computation.1 | async-start | bytes 4259840 | tf_op jit(solution)/shard_map/all_gather | solution.py:80
  14.6 5.3 %collective-permute-start = (bf16[64,512]{1,0:T(8,128)(2,1)S(1)}, bf16[64,512]{1,0:T(8,128)(2,1)S(1)}, u32[]{:S(2)}, u32[]{:S(2)}) collective-permute-start(bf16[64,512]{1,0:T(8,128)(2,1)S(1)} %fusion.89), channel_id=1, source_target_pairs={{0,64},{64,128},{128,192},{1,65},{65,129},{129,193},{2,66},{66,130... | collective-permute-start | bytes 196616 | tf_op jit(solution)/shard_map/ppermute | solution.py:14
  19.8 9.7 %copy-start.8 = (f32[7,64,512]{2,1,0:T(8,128)S(1)}, f32[7,64,512]{2,1,0:T(8,128)}, u32[]{:S(2)}) copy-start(f32[7,64,512]{2,1,0:T(8,128)} %fusion.252) | copy-start | bytes 2752516
  20.3 11.0 %copy-start.4 = (bf16[1,2,512,2048]{3,2,1,0:T(8,128)(2,1)S(1)}, bf16[1,2,512,2048]{3,2,1,0:T(8,128)(2,1)}, u32[]{:S(2)}) copy-start(bf16[1,2,512,2048]{3,2,1,0:T(8,128)(2,1)} %param.10) | copy-start | bytes 12582916
  25.8 5.0 %collective-permute-start.1 = (bf16[64,512]{1,0:T(8,128)(2,1)S(1)}, bf16[64,512]{1,0:T(8,128)(2,1)S(1)}, u32[]{:S(2)}, u32[]{:S(2)}) collective-permute-start(bf16[64,512]{1,0:T(8,128)(2,1)S(1)} %fusion.86), channel_id=1, source_target_pairs={{0,64},{64,128},{128,192},{1,65},{65,129},{129,193},{2,66},{66,130... | collective-permute-start | bytes 196616 | tf_op jit(solution)/shard_map/ppermute | solution.py:14
  32.6 6.3 %copy-start.12 = (f32[7,64,2048]{2,1,0:T(8,128)S(1)}, f32[7,64,2048]{2,1,0:T(8,128)}, u32[]{:S(2)}) copy-start(f32[7,64,2048]{2,1,0:T(8,128)} %get-tuple-element.40) | copy-start | bytes 11010052
  33.4 5.1 %collective-permute-start.2 = (bf16[64,512]{1,0:T(8,128)(2,1)S(1)}, bf16[64,512]{1,0:T(8,128)(2,1)S(1)}, u32[]{:S(2)}, u32[]{:S(2)}) collective-permute-start(bf16[64,512]{1,0:T(8,128)(2,1)S(1)} %fusion.83), channel_id=1, source_target_pairs={{0,64},{64,128},{128,192},{1,65},{65,129},{129,193},{2,66},{66,130... | collective-permute-start | bytes 196616 | tf_op jit(solution)/shard_map/ppermute | solution.py:14
  40.2 5.4 %collective-permute-start.3 = (bf16[64,512]{1,0:T(8,128)(2,1)S(1)}, bf16[64,512]{1,0:T(8,128)(2,1)S(1)}, u32[]{:S(2)}, u32[]{:S(2)}) collective-permute-start(bf16[64,512]{1,0:T(8,128)(2,1)S(1)} %fusion.80), channel_id=1, source_target_pairs={{0,64},{64,128},{128,192},{1,65},{65,129},{129,193},{2,66},{66,130... | collective-permute-start | bytes 196616 | tf_op jit(solution)/shard_map/ppermute | solution.py:14
  47.4 5.1 %collective-permute-start.4 = (bf16[64,512]{1,0:T(8,128)(2,1)S(1)}, bf16[64,512]{1,0:T(8,128)(2,1)S(1)}, u32[]{:S(2)}, u32[]{:S(2)}) collective-permute-start(bf16[64,512]{1,0:T(8,128)(2,1)S(1)} %fusion.77), channel_id=1, source_target_pairs={{0,64},{64,128},{128,192},{1,65},{65,129},{129,193},{2,66},{66,130... | collective-permute-start | bytes 196616 | tf_op jit(solution)/shard_map/ppermute | solution.py:14
  52.9 0.8 copy-start.9
  53.6 6.5 %copy-start.10 = (bf16[7,64,512]{2,1,0:T(8,128)(2,1)S(1)}, bf16[7,64,512]{2,1,0:T(8,128)(2,1)}, u32[]{:S(2)}) copy-start(bf16[7,64,512]{2,1,0:T(8,128)(2,1)} %copy-done.9) | copy-start | bytes 1376260
  53.6 7.3 %copy-start.6 = (bf16[4,64,512]{2,1,0:T(8,128)(2,1)S(1)}, bf16[4,64,512]{2,1,0:T(8,128)(2,1)}, u32[]{:S(2)}) copy-start(bf16[4,64,512]{2,1,0:T(8,128)(2,1)} %param.15) | copy-start | bytes 786436
  54.4 5.4 %collective-permute-start.5 = (bf16[64,512]{1,0:T(8,128)(2,1)S(1)}, bf16[64,512]{1,0:T(8,128)(2,1)S(1)}, u32[]{:S(2)}, u32[]{:S(2)}) collective-permute-start(bf16[64,512]{1,0:T(8,128)(2,1)S(1)} %fusion.74), channel_id=1, source_target_pairs={{0,64},{64,128},{128,192},{1,65},{65,129},{129,193},{2,66},{66,130... | collective-permute-start | bytes 196616 | tf_op jit(solution)/shard_map/ppermute | solution.py:14
  60.2 47.6 %copy-start.11 = (bf16[7,64,512]{2,1,0:T(8,128)(2,1)}, bf16[7,64,512]{2,1,0:T(8,128)(2,1)S(1)}, u32[]{:S(2)}) copy-start(bf16[7,64,512]{2,1,0:T(8,128)(2,1)S(1)} %constant_dynamic-update-slice_fusion) | copy-start | bytes 1376260
  60.8 43.8 %copy-start.13 = (f32[7,64,2048]{2,1,0:T(8,128)}, f32[7,64,2048]{2,1,0:T(8,128)S(1)}, u32[]{:S(2)}) copy-start(f32[7,64,2048]{2,1,0:T(8,128)S(1)} %get-tuple-element.48) | copy-start | bytes 11010052
  65.3 5.7 %collective-permute-start.6 = (bf16[64,512]{1,0:T(8,128)(2,1)S(1)}, bf16[64,512]{1,0:T(8,128)(2,1)S(1)}, u32[]{:S(2)}, u32[]{:S(2)}) collective-permute-start(bf16[64,512]{1,0:T(8,128)(2,1)S(1)} %fusion.285), channel_id=1, source_target_pairs={{64,0},{128,64},{192,128},{65,1},{129,65},{193,129},{66,2},{130,66... | collective-permute-start | bytes 196616 | tf_op jit(solution)/shard_map/ppermute | solution.py:14
  75.5 5.4 %collective-permute-start.7 = (bf16[64,512]{1,0:T(8,128)(2,1)S(1)}, bf16[64,512]{1,0:T(8,128)(2,1)S(1)}, u32[]{:S(2)}, u32[]{:S(2)}) collective-permute-start(bf16[64,512]{1,0:T(8,128)(2,1)S(1)} %fusion.280), channel_id=1, source_target_pairs={{64,0},{128,64},{192,128},{65,1},{129,65},{193,129},{66,2},{130,66... | collective-permute-start | bytes 196616 | tf_op jit(solution)/shard_map/ppermute | solution.py:14
  85.3 5.0 %collective-permute-start.8 = (bf16[64,512]{1,0:T(8,128)(2,1)S(1)}, bf16[64,512]{1,0:T(8,128)(2,1)S(1)}, u32[]{:S(2)}, u32[]{:S(2)}) collective-permute-start(bf16[64,512]{1,0:T(8,128)(2,1)S(1)} %fusion.275), channel_id=1, source_target_pairs={{64,0},{128,64},{192,128},{65,1},{129,65},{193,129},{66,2},{130,66... | collective-permute-start | bytes 196616 | tf_op jit(solution)/shard_map/ppermute | solution.py:14
  92.1 5.5 %collective-permute-start.9 = (bf16[64,512]{1,0:T(8,128)(2,1)S(1)}, bf16[64,512]{1,0:T(8,128)(2,1)S(1)}, u32[]{:S(2)}, u32[]{:S(2)}) collective-permute-start(bf16[64,512]{1,0:T(8,128)(2,1)S(1)} %fusion.270), channel_id=1, source_target_pairs={{64,0},{128,64},{192,128},{65,1},{129,65},{193,129},{66,2},{130,66... | collective-permute-start | bytes 196616 | tf_op jit(solution)/shard_map/ppermute | solution.py:14
  99.3 5.3 %collective-permute-start.10 = (bf16[64,512]{1,0:T(8,128)(2,1)S(1)}, bf16[64,512]{1,0:T(8,128)(2,1)S(1)}, u32[]{:S(2)}, u32[]{:S(2)}) collective-permute-start(bf16[64,512]{1,0:T(8,128)(2,1)S(1)} %fusion.265), channel_id=1, source_target_pairs={{64,0},{128,64},{192,128},{65,1},{129,65},{193,129},{66,2},{130,66... | collective-permute-start | bytes 196616 | tf_op jit(solution)/shard_map/ppermute | solution.py:14
  106.3 5.4 %collective-permute-start.11 = (bf16[64,512]{1,0:T(8,128)(2,1)S(1)}, bf16[64,512]{1,0:T(8,128)(2,1)S(1)}, u32[]{:S(2)}, u32[]{:S(2)}) collective-permute-start(bf16[64,512]{1,0:T(8,128)(2,1)S(1)} %fusion.260), channel_id=1, source_target_pairs={{64,0},{128,64},{192,128},{65,1},{129,65},{193,129},{66,2},{130,66... | collective-permute-start | bytes 196616 | tf_op jit(solution)/shard_map/ppermute | solution.py:14
  142.5 7.8 %copy-start.2 = (f32[2,512,2048]{2,1,0:T(8,128)S(1)}, f32[2,512,2048]{2,1,0:T(8,128)}, u32[]{:S(2)}) copy-start(f32[2,512,2048]{2,1,0:T(8,128)} %maximum_multiply_fusion) | copy-start | bytes 25165828
  142.5 8.9 %copy-start.5 = (bf16[1,1,2,512,2048]{4,3,2,1,0:T(8,128)(2,1)S(1)}, bf16[1,1,2,512,2048]{4,3,2,1,0:T(8,128)(2,1)}, u32[]{:S(2)}) copy-start(bf16[1,1,2,512,2048]{4,3,2,1,0:T(8,128)(2,1)} %param.13) | copy-start | bytes 12582916
  146.1 4.3 %copy-start.3 = (f32[1,1024,2048]{2,1,0:T(8,128)}, f32[1,1024,2048]{2,1,0:T(8,128)S(1)}, u32[]{:S(2)}) copy-start(f32[1,1024,2048]{2,1,0:T(8,128)S(1)} %convert_multiply_fusion) | copy-start | bytes 25165828
  155.2 118.9 %all-to-all-start = ((bf16[64,16,2048]{2,1,0:T(8,128)(2,1)}), bf16[64,16,2048]{2,1,0:T(8,128)(2,1)}, u32[]{:S(2)}, u32[]{:S(2)}) async-start(bf16[64,16,2048]{2,1,0:T(8,128)(2,1)} %multiply_convert_fusion.1), calls=%async_computation | async-start | bytes 8388608 | tf_op jit(solution)/shard_map/all_to_all | solution.py:143
  178.3 102.3 %copy-start.1 = (bf16[128,512]{1,0:T(8,128)(2,1)S(1)}, bf16[128,512]{1,0:T(8,128)(2,1)}, u32[]{:S(2)}) copy-start(bf16[128,512]{1,0:T(8,128)(2,1)} %param.9) | copy-start | bytes 393220
  188.9 88.1 %copy-start.7 = (f32[1,16,2048]{2,1,0:T(8,128)S(1)}, f32[1,16,2048]{2,1,0:T(8,128)}, u32[]{:S(2)}) copy-start(f32[1,16,2048]{2,1,0:T(8,128)} %param.14) | copy-start | bytes 393220
  188.9 90.2 %copy-start.14 = (bf16[1,16,2048]{2,1,0:T(8,128)(2,1)S(1)}, bf16[1,16,2048]{2,1,0:T(8,128)(2,1)}, u32[]{:S(2)}) copy-start(bf16[1,16,2048]{2,1,0:T(8,128)(2,1)} %param.11) | copy-start | bytes 196612
Sparse Core Ops, SparseCore 0:
  18.8 82.1 all-gather.2
where the time goes:
time: 289 us; the launch traced here: 287 us
  waiting for transfers between devices  102 us (35%)
  matrix products  62.2 us (22%)
  starting transfers between devices  54.7 us (19%)
  other arithmetic  45.8 us (16%)
  between operations  16.3 us (6%)
  local copies, waits for them, and re-layouts  6.43 us (2%)
    all_to_all x1, waiting for transfers between devices, local(): lax.all_to_all(flat.reshape(replicas, owned, channels), 'dp', split_axis=...  85.3 us
    dot_general x14, matrix products, row_product(): lax.dot_general(left, right, (((0,), (0,)), ((), ())), preferred_element_...  34.7 us
    ppermute x12, starting transfers between devices, passed_along(): return lax.ppermute(array, axis, pairs)  31.6 us
    all_to_all x1, starting transfers between devices, local(): lax.all_to_all(flat.reshape(replicas, owned, channels), 'dp', split_axis=...  23.1 us
    ppermute x12, waiting for transfers between devices, passed_along(): return lax.ppermute(array, axis, pairs)  16.8 us
    convert_element_type x1, other arithmetic, local(): (combined - packed.astype(jnp.float32)).astype(jnp.bfloat16)[None, None]  10.5 us
    dot_general x7, matrix products, forward_block(): upper = jnp.dot(normed_b, first_matrix, preferred_element_type=jnp.float32)  9.4 us
    mul x1, other arithmetic, local(): 0.1 * gradient  8.49 us
  transfers between devices with their start and end apart: 14, of which 13 were waited for; matrix products, arithmetic and copies ran while one was open for 28% of the time, Pallas kernels for 0%

commit v1 on v0

v1 whole, which is shorter than its diff:
```python
import functools
import math

import jax
import jax.numpy as jnp
from jax import lax
from jax.experimental import pallas as pl
from jax.experimental.pallas import tpu as pltpu
from jax.sharding import PartitionSpec as P

gelu_coef = math.sqrt(2.0 / math.pi)
MESH = pl.DeviceIdType.MESH
BF = jnp.bfloat16
F32 = jnp.float32
NX = 4
NC = 2


def dot_nn(a, b):
    return lax.dot_general(a, b, (((1,), (0,)), ((), ())), preferred_element_type=F32)


def dot_nt(a, b):
    return lax.dot_general(a, b, (((1,), (1,)), ((), ())), preferred_element_type=F32)


def dot_tn(a, b):
    return lax.dot_general(a, b, (((0,), (0,)), ((), ())), preferred_element_type=F32)


def step_kernel(
    ns, nz, mb, tok, d, hc, tile,
    ids_ref, embed_ref, w_hbm, var_ref, mom_hbm, we_hbm, se_ref, cot_ref,
    nw_ref, nm_ref, ne_hbm, nse_ref,
    w, own_w, we, mom, comb, packed, ne, xin, fout, gout, nf, scf, slope, left, right,
    d0, s0, ra, fa, fb, s1, zr,
    loc, f_s, f_r, b_s, b_r, gz_s, gz_r, gx_s, gx_r, gd_s, gd_r,
    d_s, d_r, a_s, a_r, ta_s, ta_r, tb_s, tb_r, z_s, z_r,
):
    s = lax.axis_index("section")
    r = lax.axis_index("dp")
    core = r % NC
    z = (r // NC) % nz
    x = r // (NC * nz)
    na = x + 1 - 2 * (x % 2)
    nb = 3 - x
    opp = (x + 2) % 4
    half = nz // 2
    ng = nz // 4

    def at(xx, zz, cc):
        return (xx * nz + zz) * NC + cc

    partner = at(x, z, 1 - core)
    dev_a = at(na, z, core)
    dev_b = at(nb, z, core)

    def dev_z(zeta):
        return at(x, (z + zeta) % nz, core)

    def remote(src, dst, send, recv, to):
        return pltpu.make_async_remote_copy(
            src_ref=src, dst_ref=dst, send_sem=send, recv_sem=recv,
            device_id={"dp": to}, device_id_type=MESH,
        )

    barrier = pltpu.get_barrier_semaphore()
    for peer in [partner, dev_a, dev_b] + [dev_z(k) for k in range(1, nz)]:
        pl.semaphore_signal(barrier, inc=1, device_id={"dp": peer}, device_id_type=MESH)

    @pl.when(s > 0)
    def _():
        pl.semaphore_signal(barrier, inc=1, device_id={"section": s - 1}, device_id_type=MESH)

    @pl.when(s < ns - 1)
    def _():
        pl.semaphore_signal(barrier, inc=1, device_id={"section": s + 1}, device_id_type=MESH)

    cp_mom = pltpu.make_async_copy(mom_hbm.at[0], mom.at[x, z, core], loc.at[0])
    cp_w0 = pltpu.make_async_copy(w_hbm.at[0, 0], w.at[0], loc.at[1])
    cp_w1 = pltpu.make_async_copy(w_hbm.at[0, 1], w.at[1], loc.at[2])
    cp_we = pltpu.make_async_copy(we_hbm, we, loc.at[3])
    cp_ow = pltpu.make_async_copy(
        w_hbm.at[0, x // 2, pl.ds(pl.multiple_of((r % (NC * nz * 2)) * 16, 16), 16)], own_w, loc.at[4]
    )
    cp_mom.start()
    cp_w0.start()
    cp_w1.start()
    cp_ow.start()
    cp_we.start()

    @pl.when(s == 0)
    def _():
        vocab = embed_ref.shape[0]
        for m in range(mb):
            hot = (
                lax.broadcasted_iota(jnp.int32, (vocab, tok), 0) == ids_ref[m : m + 1, :]
            ).astype(F32).astype(BF)
            xin[m] = dot_tn(hot, embed_ref[...]).astype(BF)

    @pl.when(s == ns - 1)
    def _():
        left[1] = cot_ref[...]

    pl.semaphore_wait(
        barrier, 2 + nz + jnp.where(s > 0, 1, 0) + jnp.where(s < ns - 1, 1, 0)
    )

    cp_mom.wait()

    def g_z(zeta):
        blk = mom.at[x, z, core]
        return remote(blk, blk, gz_s.at[zeta - 1], gz_r.at[zeta - 1], dev_z(zeta))

    def g_z_in(zeta):
        blk = mom.at[x, (z + nz - zeta) % nz, core]
        return remote(blk, blk, gz_s.at[zeta - 1], gz_r.at[zeta - 1], dev_z(zeta))

    def g_x(xx, lo, n, k, to):
        blk = mom.at[xx, pl.ds(lo, n), core]
        return remote(blk, blk, gx_s.at[k], gx_r.at[k], to)

    def g_d(xx, cc, k):
        blk = mom.at[xx, pl.ds(0, nz), cc]
        return remote(blk, blk, gd_s.at[k], gd_r.at[k], partner)

    for k in range(nz):
        zeta = half + k // 2 if k % 2 == 0 else half - 1 - k // 2
        if zeta:
            g_z(zeta).start()

    cp_w0.wait()
    cp_w1.wait()

    def send_f(m):
        return pltpu.make_async_remote_copy(
            src_ref=fout.at[m], dst_ref=xin.at[m], send_sem=f_s.at[m], recv_sem=f_r.at[m],
            device_id={"section": jnp.minimum(s + 1, ns - 1)}, device_id_type=MESH,
        )

    def send_b(m):
        return pltpu.make_async_remote_copy(
            src_ref=gout.at[m], dst_ref=left.at[1, m], send_sem=b_s.at[m], recv_sem=b_r.at[m],
            device_id={"section": jnp.maximum(s - 1, 0)}, device_id_type=MESH,
        )

    nt = hc // tile

    @pl.loop(0, 2 * (ns - 1) + mb)
    def _(t):
        mf = t - s
        mbk = t - (2 * (ns - 1) - s)

        @pl.when(t == 4 + jnp.where(s == 1, 1, 0))
        def _():
            for zeta in range(1, nz):
                g_z_in(zeta).wait_recv()
            g_x(x, 0, nz, 0, dev_a).start()
            g_x(x, 0, nz, 1, dev_b).start()
            g_d(x, core, 0).start()

        @pl.when(t == 5 + (s + 1) // 2)
        def _():
            g_x(na, 0, nz, 0, dev_a).wait_recv()
            g_x(nb, 0, nz, 1, dev_b).wait_recv()
            g_x(nb, 0, half, 2, dev_a).start()
            g_x(na, half, half, 3, dev_b).start()
            g_d(na, core, 1).start()
            g_d(nb, core, 2).start()

        @pl.when(t == 2 * (ns - 1) + mb - 1)
        def _():
            g_x(opp, 0, half, 2, dev_a).wait_recv()
            g_x(opp, half, half, 3, dev_b).wait_recv()
            g_d(opp, core, 3).start()

        @pl.when(jnp.logical_and(mf >= 0, mf < mb))
        def _():
            @pl.when(s > 0)
            def _():
                send_f(mf).wait_recv()

            xv = xin[mf].astype(F32)
            center = jnp.mean(xv, axis=-1, keepdims=True)
            dev = xv - center
            spread = jnp.mean(dev * dev, axis=-1, keepdims=True)
            scaled = lax.rsqrt(spread + 1e-05)
            normed = dev * scaled
            nf[mf] = normed
            scf[mf] = jnp.broadcast_to(scaled, (tok, 128))
            nbv = normed.astype(BF)
            left[0, mf] = nbv
            acc = xv
            for j in range(nt):
                cols = slice(j * tile, (j + 1) * tile)
                u = dot_nn(nbv, w[0, :, cols])
                uu = u * u
                bent = jnp.tanh(u * (gelu_coef + (gelu_coef * 0.044715) * uu))
                hu = 0.5 * u
                hp = 0.5 + 0.5 * bent
                hid = (u * hp).astype(BF)
                right[1, mf, :, cols] = hid
                slope[mf, :, cols] = hp + hu * (1.0 - bent * bent) * (
                    gelu_coef + (gelu_coef * 3.0 * 0.044715) * uu
                )
                acc = acc + dot_nt(hid, w[1, :, cols])

            @pl.when(s < ns - 1)
            def _():
                fout[mf] = acc.astype(BF)
                send_f(mf).start()

        @pl.when(jnp.logical_and(mbk >= 0, mbk < mb))
        def _():
            @pl.when(s < ns - 1)
            def _():
                send_b(mbk).wait_recv()

            g = left[1, mbk]
            for j in range(nt):
                cols = slice(j * tile, (j + 1) * tile)
                bh = dot_nn(g, w[1, :, cols])
                right[0, mbk, :, cols] = (bh * slope[mbk, :, cols]).astype(BF)

            @pl.when(s > 0)
            def _():
                bn = dot_nt(right[0, mbk], w[0])
                normed = nf[mbk]
                first = jnp.mean(bn, axis=-1, keepdims=True)
                second = jnp.mean(bn * normed, axis=-1, keepdims=True)
                sc = scf[mbk][:, :1]
                gout[mbk] = (g.astype(F32) + sc * (bn - first - normed * second)).astype(BF)
                send_b(mbk).start()

    cp_we.wait()
    for k, xx in enumerate((x, na, nb, opp)):
        g_d(xx, 1 - core, k).wait_recv()

    qx = NX // 2
    ct = 512 if hc % 512 == 0 else 256
    nct = hc // ct
    rows = qx * nz * NC * 16

    def first_pass(idx, sq):
        i = idx // nct
        j = pl.multiple_of((idx % nct) * ct, ct)
        lt = left[i].reshape(mb * tok, d)
        rt = right[i, :, :, pl.ds(j, ct)].reshape(mb * tok, ct)
        grad = dot_tn(lt, rt)
        shared = mom[pl.ds(i * qx, qx), :, :, :, pl.ds(j, ct)].reshape(rows, ct).astype(F32)
        err = we[pl.ds(i * qx, qx), :, :, :, pl.ds(j, ct)].reshape(rows, ct).astype(F32)
        c = 0.9 * shared + 0.1 * grad + err
        comb[pl.ds(i * qx, qx), :, :, :, pl.ds(j, ct)] = c.reshape(qx, nz, NC, 16, ct)
        return sq + jnp.sum((c * c).reshape(rows // 8, 8, ct), axis=0)

    sq = lax.fori_loop(0, 2 * nct, first_pass, jnp.zeros((8, ct), F32))
    total_sq = jnp.sum(jnp.sum(sq, axis=0, keepdims=True), axis=1, keepdims=True)
    scale = jnp.sqrt(total_sq * (1.0 / (2 * d * hc)) + 0.01)
    inverse = 1.0 / scale

    def second_pass(q):
        @pl.loop(0, nz)
        def _(k):
            c = comb[q, k].reshape(NC * 16, hc)
            p = (scale * jnp.tanh(c * inverse)).astype(BF)
            packed[q, k] = p.reshape(NC, 16, hc)
            ne[q, k] = (c - p.astype(F32)).astype(BF).reshape(NC, 16, hc)

    def cp_ne(q, k):
        return pltpu.make_async_copy(ne.at[q], ne_hbm.at[q], loc.at[5 + k])

    def to_partner(q, k):
        return remote(packed.at[q, pl.ds(0, nz), 1 - core], d0.at[k], d_s.at[k], d_r.at[k], partner)

    def pair_sum(q, k):
        to_partner(q, k).wait_recv()

        @pl.loop(0, nz)
        def _(i):
            zeta = half + i // 2 - (i % 2) * (1 + 2 * (i // 2))
            zz = (z + zeta) % nz
            s0[k, i] = (packed[q, zz, core].astype(F32) + d0[k, zz].astype(F32)).astype(BF)

    def grp(ref, g):
        return ref.at[pl.ds(g * ng, ng)]

    def send_opp(g):
        to = dev_a if g % 2 == 0 else dev_b
        return remote(grp(s0.at[0], g), grp(ra, g), a_s.at[g], a_r.at[g], to)

    def send_a(g):
        return remote(grp(s0.at[1], g), grp(fa, g), ta_s.at[g], ta_r.at[g], dev_a)

    def send_bb(g):
        return remote(grp(s0.at[2], g), grp(fb, g), tb_s.at[g], tb_r.at[g], dev_b)

    def augment(g):
        send_opp(g).wait_recv()
        slot = 2 if g % 2 == 0 else 1

        @pl.loop(0, ng)
        def _(i):
            k = g * ng + i
            s0[slot, k] = (s0[slot, k].astype(F32) + ra[k].astype(F32)).astype(BF)

        (send_bb if slot == 2 else send_a)(g).start()

    def z_of(k):
        return half + k // 2 if k % 2 == 0 else half - 1 - k // 2

    def send_z(k):
        return remote(s1.at[k], zr.at[k], z_s.at[k], z_r.at[k], dev_z(z_of(k)))

    def along_z(groups):
        for g in groups:
            send_a(g).wait_recv()
            send_bb(g).wait_recv()
            for i in range(ng):
                k = g * ng + i
                s1[k] = (s0[3, k].astype(F32) + fa[k].astype(F32) + fb[k].astype(F32)).astype(BF)
                if z_of(k):
                    send_z(k).start()

    second_pass(opp)
    to_partner(opp, 0).start()
    cp_ne(opp, 0).start()
    second_pass(na)
    to_partner(na, 1).start()
    cp_ne(na, 1).start()
    pair_sum(opp, 0)
    send_opp(0).start()
    send_opp(1).start()
    second_pass(nb)
    to_partner(nb, 2).start()
    cp_ne(nb, 2).start()
    pair_sum(na, 1)
    send_a(0).start()
    second_pass(x)
    to_partner(x, 3).start()
    cp_ne(x, 3).start()
    pair_sum(nb, 2)
    send_bb(1).start()
    send_opp(2).start()
    send_opp(3).start()
    augment(0)
    augment(1)
    send_a(2).start()
    send_bb(3).start()
    pair_sum(x, 3)
    augment(2)
    augment(3)
    along_z((0, 1))
    along_z((2, 3))

    total = s1[nz - 1].astype(F32)
    for k in range(nz - 1):
        send_z(k).wait_recv()
        total = total + zr[k].astype(F32)
    merged = total * (1.0 / (NX * nz * NC)) + se_ref[0]
    msq = jnp.sum(jnp.sum(merged * merged, axis=0, keepdims=True), axis=1, keepdims=True)
    sscale = jnp.sqrt(msq * (1.0 / (16 * hc)) + 0.01)
    values = (sscale * jnp.tanh(merged * (1.0 / sscale))).astype(BF)
    vf = values.astype(F32)
    nm_ref[0] = values
    nse_ref[0] = merged - vf
    cp_ow.wait()
    step = 0.01 * vf / (jnp.sqrt(var_ref[0].astype(F32)) + 1e-08)
    nw_ref[0] = (own_w[...].astype(F32) - step).astype(BF)

    for m in range(mb):
        @pl.when(s < ns - 1)
        def _():
            send_f(m).wait_send()

        @pl.when(s > 0)
        def _():
            send_b(m).wait_send()

    for zeta in range(1, nz):
        g_z(zeta).wait_send()
    g_x(x, 0, nz, 0, dev_a).wait_send()
    g_x(x, 0, nz, 1, dev_b).wait_send()
    g_x(nb, 0, half, 2, dev_a).wait_send()
    g_x(na, half, half, 3, dev_b).wait_send()
    for k, xx in enumerate((x, na, nb, opp)):
        g_d(xx, core, k).wait_send()
    for k, q in enumerate((opp, na, nb, x)):
        to_partner(q, k).wait_send()
        cp_ne(q, k).wait()
    for g in range(4):
        send_opp(g).wait_send()
        send_a(g).wait_send()
        send_bb(g).wait_send()
    for k in range(nz - 1):
        send_z(k).wait_send()


def local(ns, nz, token_ids, embed, weights, variance, momentum, worker_error, server_error, cotangent):
    mb, tok = token_ids.shape
    d = embed.shape[1]
    hc = weights.shape[3]
    dims = (NX, nz, NC, 16, hc)
    vm = pl.BlockSpec(memory_space=pltpu.VMEM)
    hbm = pl.BlockSpec(memory_space=pl.ANY)
    dma = pltpu.SemaphoreType.DMA
    tile = 512 if hc % 512 == 0 else 128
    kernel = functools.partial(step_kernel, ns, nz, mb, tok, d, hc, tile)
    nw, nm, ne, nse = pl.pallas_call(
        kernel,
        out_shape=(
            jax.ShapeDtypeStruct((1, 16, hc), BF),
            jax.ShapeDtypeStruct((1, 16, hc), BF),
            jax.ShapeDtypeStruct(dims, BF),
            jax.ShapeDtypeStruct((1, 16, hc), F32),
        ),
        in_specs=[vm, vm, hbm, vm, hbm, hbm, vm, vm],
        out_specs=(vm, vm, hbm, vm),
        scratch_shapes=[
            pltpu.VMEM((2, d, hc), BF),
            pltpu.VMEM((16, hc), BF),
            pltpu.VMEM(dims, BF),
            pltpu.VMEM(dims, BF),
            pltpu.VMEM(dims, F32),
            pltpu.VMEM(dims, BF),
            pltpu.VMEM(dims, BF),
            pltpu.VMEM((mb, tok, d), BF),
            pltpu.VMEM((mb, tok, d), BF),
            pltpu.VMEM((mb, tok, d), BF),
            pltpu.VMEM((mb, tok, d), F32),
            pltpu.VMEM((mb, tok, 128), F32),
            pltpu.VMEM((mb, tok, hc), F32),
            pltpu.VMEM((2, mb, tok, d), BF),
            pltpu.VMEM((2, mb, tok, hc), BF),
            pltpu.VMEM((4, nz, 16, hc), BF),
            pltpu.VMEM((4, nz, 16, hc), BF),
            pltpu.VMEM((nz, 16, hc), BF),
            pltpu.VMEM((nz, 16, hc), BF),
            pltpu.VMEM((nz, 16, hc), BF),
            pltpu.VMEM((nz, 16, hc), BF),
            pltpu.VMEM((nz, 16, hc), BF),
            dma((9,)),
            dma((mb,)), dma((mb,)), dma((mb,)), dma((mb,)),
            dma((nz - 1,)), dma((nz - 1,)), dma((4,)), dma((4,)), dma((4,)), dma((4,)),
            dma((4,)), dma((4,)), dma((4,)), dma((4,)), dma((4,)), dma((4,)), dma((4,)), dma((4,)),
            dma((nz,)), dma((nz,)),
        ],
        compiler_params=pltpu.CompilerParams(
            collective_id=0, has_side_effects=True, vmem_limit_bytes=60 * 1024 * 1024
        ),
        name="step",
    )(
        token_ids, embed, weights, variance, momentum,
        worker_error.reshape(dims), server_error, cotangent,
    )
    return (nw, nm, ne.reshape(worker_error.shape), nse)


def solution(mesh):
    ns = mesh.shape["section"]
    nz = mesh.shape["dp"] // (NX * NC)
    in_specs = (
        P(None, "dp"),
        P(),
        P("section", None, None, None),
        P("section", "dp", None),
        P("section", "dp", None),
        P("section", "dp", None, None, None),
        P("section", "dp", None),
        P(None, "dp", None),
    )
    out_specs = (
        P("section", "dp", None),
        P("section", "dp", None),
        P("section", "dp", None, None, None),
        P("section", "dp", None),
    )
    return jax.shard_map(
        functools.partial(local, ns, nz), mesh=mesh, in_specs=in_specs, out_specs=out_specs,
        check_vma=False,
    )
```

time: 289 us -> 97.7 us (0.34)
  waiting for transfers between devices: 102 us -> 0 us
  Pallas kernels: 0 us -> 88.5 us
  matrix products: 62.2 us -> 0 us
  starting transfers between devices: 54.7 us -> 0 us
  other arithmetic: 45.8 us -> 0 us
  between operations: 16.3 us -> 0.64 us
    pallas_call x0 -> x1, Pallas kernels: none -> 88.5 us  [local(): pl.pallas_call(kernel, out_shape=(jax.ShapeDtypeStruct((1, 16, hc), BF),...]
    all_to_all x1 -> x0, waiting for transfers between devices: 85.3 us -> none  [local(): lax.all_to_all(flat.reshape(replicas, owned, channels), 'dp', split_axis=...]
    dot_general x40 -> x0, matrix products: 62.2 us -> none  [the longest x14 34.7 us: row_product(): lax.dot_general(left, right, (((0,), (0,)), ((), ())), preferred_element_...]
    ppermute x12 -> x0, starting transfers between devices: 31.6 us -> none  [passed_along(): return lax.ppermute(array, axis, pairs)]
    all_to_all x1 -> x0, starting transfers between devices: 23.1 us -> none  [local(): lax.all_to_all(flat.reshape(replicas, owned, channels), 'dp', split_axis=...]
    ppermute x12 -> x0, waiting for transfers between devices: 16.8 us -> none  [passed_along(): return lax.ppermute(array, axis, pairs)]
    convert_element_type x8 -> x0, other arithmetic: 15 us -> none  [the longest x1 10.5 us: local(): (combined - packed.astype(jnp.float32)).astype(jnp.bfloat16)[None, None]]
    reduce_sum x17 -> x0, other arithmetic: 13.2 us -> none  [the longest x1 7.57 us: local(): worker_scale = jnp.sqrt(jnp.mean(combined * combined) + 0.01)]
  transfers between devices with their start and end apart: 14 -> 0, of which waited for: 13 -> 0; matrix products, arithmetic and copies ran while one was open for 28% -> 0% of each run, Pallas kernels for 0% -> 0%
where the time goes in v1:
time: 97.7 us; the launch traced here: 97.6 us
  Pallas kernels  88.5 us (91%)
  local copies, waits for them, and re-layouts  8.43 us (9%)
    pallas_call x1, Pallas kernels, local(): pl.pallas_call(kernel, out_shape=(jax.ShapeDtypeStruct((1, 16, hc), BF),...  88.5 us
    unnamed x6, local copies, waits for them, and re-layouts  8.43 us

profile of v1, /device:TPU:1, one launch (start us, length us, event | category | flops | bytes accessed | tf_op | source)
XLA Modules:
  0.0 97.6 jit_solution(833888401049887231)
XLA Ops:
  0.6 88.5 %step.1 = (bf16[1,16,2048]{2,1,0:T(8,128)(2,1)}, bf16[1,16,2048]{2,1,0:T(8,128)(2,1)}, bf16[4,8,2,16,2048]{4,3,2,1,0:T(8,128)(2,1)}, f32[1,16,2048]{2,1,0:T(8,128)}) custom-call(s32[4,64]{1,0:T(4,128)} %ids_ref.1, bf16[128,512]{1,0:T(8,128)(2,1)} %embed_ref.1, bf16[1,2,512,2048]{3,2,1,0:T(8,128)(2,1)} %w_hbm.1, bf16[1,16,2048]{2,1,0:T(8,128)(2,1)} %var_ref.1, ...), custom_call_target="tpu_custom_call" | custom-call | tf_op jit(solution)/shard_map/step/pallas_call | solution.py:408
  89.1 1.5 %copy.16 = bf16[1,16,2048]{2,1,0:T(8,128)(2,1)} copy(bf16[1,16,2048]{2,1,0:T(8,128)(2,1)} %get-tuple-element.16) | data formatting | bytes 131072
  90.6 1.5 %copy.17 = bf16[1,16,2048]{2,1,0:T(8,128)(2,1)} copy(bf16[1,16,2048]{2,1,0:T(8,128)(2,1)} %get-tuple-element.17) | data formatting | bytes 131072
  92.1 0.0 copy-start
  92.1 4.8 %copy.18 = bf16[1,1,2,512,2048]{4,3,2,1,0:T(8,128)(2,1)} copy(bf16[1,1,2,512,2048]{4,3,2,1,0:T(8,128)(2,1)} %bitcast.3) | data formatting | bytes 8388608
  96.9 0.0 copy-done
  96.9 0.7 copy.19
Async XLA Ops:
  92.1 4.8 %copy-start = (f32[1,16,2048]{2,1,0:T(8,128)S(1)}, f32[1,16,2048]{2,1,0:T(8,128)}, u32[]{:S(2)}) copy-start(f32[1,16,2048]{2,1,0:T(8,128)} %get-tuple-element.19) | copy-start | bytes 393220

commit v2 on v1

--- a/solution.py
+++ b/solution.py
@@ -30,9 +30,9 @@
 
 def step_kernel(
     ns, nz, mb, tok, d, hc, tile,
-    ids_ref, embed_ref, w_hbm, var_ref, mom_hbm, we_hbm, se_ref, cot_ref,
-    nw_ref, nm_ref, ne_hbm, nse_ref,
-    w, own_w, we, mom, comb, packed, ne, xin, fout, gout, nf, scf, slope, left, right,
+    ids_hbm, embed_hbm, w_hbm, var_hbm, mom_hbm, we_hbm, se_hbm, cot_hbm,
+    nw_ref, nm_ref, ne, nse_ref,
+    ids, embed, var, se, w, own_w, we, mom, comb, packed, xin, fout, gout, nf, scf, slope, left, right,
     d0, s0, ra, fa, fb, s1, zr,
     loc, f_s, f_r, b_s, b_r, gz_s, gz_r, gx_s, gx_r, gd_s, gd_r,
     d_s, d_r, a_s, a_r, ta_s, ta_r, tb_s, tb_r, z_s, z_r,
@@ -83,24 +83,44 @@
     cp_ow = pltpu.make_async_copy(
         w_hbm.at[0, x // 2, pl.ds(pl.multiple_of((r % (NC * nz * 2)) * 16, 16), 16)], own_w, loc.at[4]
     )
+    cp_ids = pltpu.make_async_copy(ids_hbm, ids, loc.at[5])
+    cp_embed = pltpu.make_async_copy(embed_hbm, embed, loc.at[6])
+    cp_var = pltpu.make_async_copy(var_hbm, var, loc.at[7])
+    cp_se = pltpu.make_async_copy(se_hbm, se, loc.at[8])
+    cp_cot = pltpu.make_async_copy(cot_hbm, left.at[1], loc.at[9])
     cp_mom.start()
+
+    @pl.when(s == 0)
+    def _():
+        cp_ids.start()
+        cp_embed.start()
+
     cp_w0.start()
     cp_w1.start()
+
+    @pl.when(s == ns - 1)
+    def _():
+        cp_cot.start()
+
+    cp_we.start()
     cp_ow.start()
-    cp_we.start()
+    cp_var.start()
+    cp_se.start()
 
     @pl.when(s == 0)
     def _():
-        vocab = embed_ref.shape[0]
+        vocab = embed.shape[0]
+        cp_ids.wait()
+        cp_embed.wait()
         for m in range(mb):
             hot = (
-                lax.broadcasted_iota(jnp.int32, (vocab, tok), 0) == ids_ref[m : m + 1, :]
+                lax.broadcasted_iota(jnp.int32, (vocab, tok), 0) == ids[m : m + 1, :]
             ).astype(F32).astype(BF)
-            xin[m] = dot_tn(hot, embed_ref[...]).astype(BF)
+            xin[m] = dot_tn(hot, embed[...]).astype(BF)
 
     @pl.when(s == ns - 1)
     def _():
-        left[1] = cot_ref[...]
+        cp_cot.wait()
 
     pl.semaphore_wait(
         barrier, 2 + nz + jnp.where(s > 0, 1, 0) + jnp.where(s < ns - 1, 1, 0)
@@ -233,6 +253,9 @@
                 send_b(mbk).start()
 
     cp_we.wait()
+    cp_ow.wait()
+    cp_var.wait()
+    cp_se.wait()
     for k, xx in enumerate((x, na, nb, opp)):
         g_d(xx, 1 - core, k).wait_recv()
 
@@ -266,9 +289,6 @@
             packed[q, k] = p.reshape(NC, 16, hc)
             ne[q, k] = (c - p.astype(F32)).astype(BF).reshape(NC, 16, hc)
 
-    def cp_ne(q, k):
-        return pltpu.make_async_copy(ne.at[q], ne_hbm.at[q], loc.at[5 + k])
-
     def to_partner(q, k):
         return remote(packed.at[q, pl.ds(0, nz), 1 - core], d0.at[k], d_s.at[k], d_r.at[k], partner)
 
@@ -323,21 +343,17 @@
 
     second_pass(opp)
     to_partner(opp, 0).start()
-    cp_ne(opp, 0).start()
     second_pass(na)
     to_partner(na, 1).start()
-    cp_ne(na, 1).start()
     pair_sum(opp, 0)
     send_opp(0).start()
     send_opp(1).start()
     second_pass(nb)
     to_partner(nb, 2).start()
-    cp_ne(nb, 2).start()
     pair_sum(na, 1)
     send_a(0).start()
     second_pass(x)
     to_partner(x, 3).start()
-    cp_ne(x, 3).start()
     pair_sum(nb, 2)
     send_bb(1).start()
     send_opp(2).start()
@@ -356,15 +372,14 @@
     for k in range(nz - 1):
         send_z(k).wait_recv()
         total = total + zr[k].astype(F32)
-    merged = total * (1.0 / (NX * nz * NC)) + se_ref[0]
+    merged = total * (1.0 / (NX * nz * NC)) + se[0]
     msq = jnp.sum(jnp.sum(merged * merged, axis=0, keepdims=True), axis=1, keepdims=True)
     sscale = jnp.sqrt(msq * (1.0 / (16 * hc)) + 0.01)
     values = (sscale * jnp.tanh(merged * (1.0 / sscale))).astype(BF)
     vf = values.astype(F32)
     nm_ref[0] = values
     nse_ref[0] = merged - vf
-    cp_ow.wait()
-    step = 0.01 * vf / (jnp.sqrt(var_ref[0].astype(F32)) + 1e-08)
+    step = 0.01 * vf / (jnp.sqrt(var[0].astype(F32)) + 1e-08)
     nw_ref[0] = (own_w[...].astype(F32) - step).astype(BF)
 
     for m in range(mb):
@@ -386,13 +401,23 @@
         g_d(xx, core, k).wait_send()
     for k, q in enumerate((opp, na, nb, x)):
         to_partner(q, k).wait_send()
-        cp_ne(q, k).wait()
     for g in range(4):
         send_opp(g).wait_send()
         send_a(g).wait_send()
         send_bb(g).wait_send()
     for k in range(nz - 1):
         send_z(k).wait_send()
+
+
+def store_kernel(a, b, c, e, a_out, b_out, c_out, e_out, sems):
+    copies = [
+        pltpu.make_async_copy(src, dst, sems.at[k])
+        for k, (src, dst) in enumerate(((c, c_out), (e, e_out), (a, a_out), (b, b_out)))
+    ]
+    for copy in copies:
+        copy.start()
+    for copy in copies:
+        copy.wait()
 
 
 def local(ns, nz, token_ids, embed, weights, variance, momentum, worker_error, server_error, cotangent):
@@ -408,20 +433,23 @@
     nw, nm, ne, nse = pl.pallas_call(
         kernel,
         out_shape=(
-            jax.ShapeDtypeStruct((1, 16, hc), BF),
-            jax.ShapeDtypeStruct((1, 16, hc), BF),
-            jax.ShapeDtypeStruct(dims, BF),
-            jax.ShapeDtypeStruct((1, 16, hc), F32),
+            pltpu.VMEM((1, 16, hc), BF),
+            pltpu.VMEM((1, 16, hc), BF),
+            pltpu.VMEM(dims, BF),
+            pltpu.VMEM((1, 16, hc), F32),
         ),
-        in_specs=[vm, vm, hbm, vm, hbm, hbm, vm, vm],
-        out_specs=(vm, vm, hbm, vm),
+        in_specs=[hbm] * 8,
+        out_specs=(vm, vm, vm, vm),
         scratch_shapes=[
+            pltpu.VMEM((mb, tok), jnp.int32),
+            pltpu.VMEM(embed.shape, BF),
+            pltpu.VMEM((1, 16, hc), BF),
+            pltpu.VMEM((1, 16, hc), F32),
             pltpu.VMEM((2, d, hc), BF),
             pltpu.VMEM((16, hc), BF),
             pltpu.VMEM(dims, BF),
             pltpu.VMEM(dims, BF),
             pltpu.VMEM(dims, F32),
-            pltpu.VMEM(dims, BF),
             pltpu.VMEM(dims, BF),
             pltpu.VMEM((mb, tok, d), BF),
             pltpu.VMEM((mb, tok, d), BF),
@@ -438,20 +466,33 @@
             pltpu.VMEM((nz, 16, hc), BF),
             pltpu.VMEM((nz, 16, hc), BF),
             pltpu.VMEM((nz, 16, hc), BF),
-            dma((9,)),
+            dma((10,)),
             dma((mb,)), dma((mb,)), dma((mb,)), dma((mb,)),
             dma((nz - 1,)), dma((nz - 1,)), dma((4,)), dma((4,)), dma((4,)), dma((4,)),
             dma((4,)), dma((4,)), dma((4,)), dma((4,)), dma((4,)), dma((4,)), dma((4,)), dma((4,)),
             dma((nz,)), dma((nz,)),
         ],
         compiler_params=pltpu.CompilerParams(
-            collective_id=0, has_side_effects=True, vmem_limit_bytes=60 * 1024 * 1024
+            collective_id=0, has_side_effects=True, vmem_limit_bytes=48 * 1024 * 1024
         ),
         name="step",
-    )(
-        token_ids, embed, weights, variance, momentum,
-        worker_error.reshape(dims), server_error, cotangent,
-    )
+    )(*(
+        pltpu.with_memory_space_constraint(a, pltpu.MemorySpace.HBM)
+        for a in (
+            token_ids, embed, weights, variance, momentum,
+            worker_error.reshape(dims), server_error, cotangent,
+        )
+    ))
+    arrays = (nw, nm, ne, nse)
+    nw, nm, ne, nse = pl.pallas_call(
+        store_kernel,
+        out_shape=tuple(jax.ShapeDtypeStruct(a.shape, a.dtype) for a in arrays),
+        in_specs=[vm] * 4,
+        out_specs=(hbm,) * 4,
+        scratch_shapes=[dma((4,))],
+        compiler_params=pltpu.CompilerParams(vmem_limit_bytes=4 * 1024 * 1024),
+        name="store",
+    )(*(pltpu.with_memory_space_constraint(a, pltpu.MemorySpace.VMEM) for a in arrays))
     return (nw, nm, ne.reshape(worker_error.shape), nse)
 
 

time: 97.7 us -> 89.7 us (0.918)
  local copies, waits for them, and re-layouts: 8.43 us -> 0 us
    unnamed x6 -> x0, local copies, waits for them, and re-layouts: 8.43 us -> none
    pallas_call x1 -> x2, Pallas kernels: 88.5 us -> 88.9 us  [the longest x1 86.8 us: local(): pl.pallas_call(kernel, out_shape=(pltpu.VMEM((1, 16, hc), BF), pltpu.VMEM...]
where the time goes in v2:
time: 89.7 us; the launch traced here: 89.6 us
  Pallas kernels  88.9 us (99%)
    pallas_call x1, Pallas kernels, local(): pl.pallas_call(kernel, out_shape=(pltpu.VMEM((1, 16, hc), BF), pltpu.VMEM...  86.8 us
    pallas_call x1, Pallas kernels, local(): pl.pallas_call(store_kernel, out_shape=tuple((jax.ShapeDtypeStruct(a.shap...  2.11 us

profile of v2, /device:TPU:1, one launch (start us, length us, event | category | flops | bytes accessed | tf_op | source)
XLA Modules:
  0.0 89.6 jit_solution(15873328606170041008)
XLA Ops:
  0.6 86.8 %step.1 = (bf16[1,16,2048]{2,1,0:T(8,128)(2,1)S(1)}, bf16[1,16,2048]{2,1,0:T(8,128)(2,1)S(1)}, bf16[4,8,2,16,2048]{4,3,2,1,0:T(8,128)(2,1)S(1)}, f32[1,16,2048]{2,1,0:T(8,128)S(1)}) custom-call(s32[4,64]{1,0:T(4,128)} %ids_hbm.1, bf16[128,512]{1,0:T(8,128)(2,1)} %embed_hbm.1, bf16[1,2,512,2048]{3,2,1,0:T(8,128)(2,1)} %w_hbm.1, bf16[1,16,2048]{2,1,0:T(8,128)(2,1)} %var_hbm.1, ...), custom_call_target="tpu_custom_call" | custom-call | tf_op jit(solution)/shard_map/step/pallas_call | solution.py:433
  87.5 2.1 %store.1 = (bf16[1,16,2048]{2,1,0:T(8,128)(2,1)}, bf16[1,16,2048]{2,1,0:T(8,128)(2,1)}, bf16[4,8,2,16,2048]{4,3,2,1,0:T(8,128)(2,1)}, f32[1,16,2048]{2,1,0:T(8,128)}) custom-call(bf16[1,16,2048]{2,1,0:T(8,128)(2,1)S(1)} %get-tuple-element.12.a, bf16[1,16,2048]{2,1,0:T(8,128)(2,1)S(1)} %get-tuple-element.13.b, ...), custom_call_target="tpu_custom_call" | custom-call | tf_op jit(solution)/shard_map/store/pallas_call | solution.py:487

commit v3 on v2

--- a/solution.py
+++ b/solution.py
@@ -32,9 +32,9 @@
     ns, nz, mb, tok, d, hc, tile,
     ids_hbm, embed_hbm, w_hbm, var_hbm, mom_hbm, we_hbm, se_hbm, cot_hbm,
     nw_ref, nm_ref, ne, nse_ref,
-    ids, embed, var, se, w, own_w, we, mom, comb, packed, xin, fout, gout, nf, scf, slope, left, right,
+    ids, embed, var, se, w, wt, own_w, we, mom, comb, packed, xin, fout, gout, nf, scf, slope, left, right,
     d0, s0, ra, fa, fb, s1, zr,
-    loc, f_s, f_r, b_s, b_r, gz_s, gz_r, gx_s, gx_r, gd_s, gd_r,
+    loc, f_s, f_r, b_s, b_r, gz_s, gz_r, gx_s, gx_r, gy_s, gy_r, gd_s, gd_r,
     d_s, d_r, a_s, a_r, ta_s, ta_r, tb_s, tb_r, z_s, z_r,
 ):
     s = lax.axis_index("section")
@@ -46,7 +46,6 @@
     nb = 3 - x
     opp = (x + 2) % 4
     half = nz // 2
-    ng = nz // 4
 
     def at(xx, zz, cc):
         return (xx * nz + zz) * NC + cc
@@ -88,21 +87,19 @@
     cp_var = pltpu.make_async_copy(var_hbm, var, loc.at[7])
     cp_se = pltpu.make_async_copy(se_hbm, se, loc.at[8])
     cp_cot = pltpu.make_async_copy(cot_hbm, left.at[1], loc.at[9])
-    cp_mom.start()
-
     @pl.when(s == 0)
     def _():
         cp_ids.start()
         cp_embed.start()
 
+    cp_w1.start()
     cp_w0.start()
-    cp_w1.start()
+    cp_mom.start()
 
     @pl.when(s == ns - 1)
     def _():
         cp_cot.start()
 
-    cp_we.start()
     cp_ow.start()
     cp_var.start()
     cp_se.start()
@@ -118,39 +115,81 @@
             ).astype(F32).astype(BF)
             xin[m] = dot_tn(hot, embed[...]).astype(BF)
 
+    def transposed(i):
+        step = 256 if hc % 256 == 0 else hc
+
+        @pl.loop(0, hc // step)
+        def _(j):
+            lo = pl.multiple_of(j * step, step)
+            wt[i, pl.ds(lo, step), :] = w[i, :, pl.ds(lo, step)].T
+
     @pl.when(s == ns - 1)
     def _():
         cp_cot.wait()
 
+    cp_w1.wait()
+    transposed(1)
+    cp_w0.wait()
+
     pl.semaphore_wait(
         barrier, 2 + nz + jnp.where(s > 0, 1, 0) + jnp.where(s < ns - 1, 1, 0)
     )
 
     cp_mom.wait()
-
-    def g_z(zeta):
+    order = [0]
+    for dist in range(1, half):
+        order += [dist, nz - dist]
+    order.append(half)
+    parts = (range(0, half + 1), range(half + 1, nz))
+
+    def mom_at(xx, k):
+        return mom.at[xx, (z + order[k]) % nz, core]
+
+    def g_z(k):
         blk = mom.at[x, z, core]
-        return remote(blk, blk, gz_s.at[zeta - 1], gz_r.at[zeta - 1], dev_z(zeta))
-
-    def g_z_in(zeta):
-        blk = mom.at[x, (z + nz - zeta) % nz, core]
-        return remote(blk, blk, gz_s.at[zeta - 1], gz_r.at[zeta - 1], dev_z(zeta))
-
-    def g_x(xx, lo, n, k, to):
-        blk = mom.at[xx, pl.ds(lo, n), core]
-        return remote(blk, blk, gx_s.at[k], gx_r.at[k], to)
-
-    def g_d(xx, cc, k):
-        blk = mom.at[xx, pl.ds(0, nz), cc]
-        return remote(blk, blk, gd_s.at[k], gd_r.at[k], partner)
-
-    for k in range(nz):
-        zeta = half + k // 2 if k % 2 == 0 else half - 1 - k // 2
-        if zeta:
-            g_z(zeta).start()
-
-    cp_w0.wait()
-    cp_w1.wait()
+        return remote(blk, blk, gz_s.at[k], gz_r.at[order.index((nz - order[k]) % nz)], dev_z(order[k]))
+
+    def g_z_in(k):
+        blk = mom_at(x, k)
+        return remote(blk, blk, gz_s.at[k], gz_r.at[k], dev_z(order[k]))
+
+    def g_x(xx, k, j):
+        blk = mom_at(xx, k)
+        return remote(blk, blk, gx_s.at[j, k], gx_r.at[j, k], (dev_a, dev_b)[j])
+
+    def g_y(xx, k):
+        blk = mom_at(xx, k)
+        return remote(blk, blk, gy_s.at[k], gy_r.at[k], (dev_a, dev_b)[k % 2])
+
+    def g_d(j, xx, k, cc):
+        blk = mom.at[xx, (z + order[k]) % nz, cc]
+        return remote(blk, blk, gd_s.at[j, k], gd_r.at[j, k], partner)
+
+    for k in range(1, nz):
+        g_z(k).start()
+
+    cp_we.start()
+
+    def from_z(part):
+        for k in parts[part]:
+            if k:
+                g_z_in(k).wait_recv()
+            g_x(x, k, 0).start()
+            g_x(x, k, 1).start()
+            g_d(0, x, k, core).start()
+
+    def from_x(part):
+        for k in parts[part]:
+            g_x(na, k, 0).wait_recv()
+            g_x(nb, k, 1).wait_recv()
+            g_y(nb if k % 2 == 0 else na, k).start()
+            g_d(1, na, k, core).start()
+            g_d(2, nb, k, core).start()
+
+    def from_far():
+        for k in range(nz):
+            g_y(opp, k).wait_recv()
+            g_d(3, opp, k, core).start()
 
     def send_f(m):
         return pltpu.make_async_remote_copy(
@@ -166,33 +205,45 @@
 
     nt = hc // tile
 
-    @pl.loop(0, 2 * (ns - 1) + mb)
+    slots = 2 * (ns - 1) + mb
+    first_b = jnp.where(s == ns - 1, ns - 1, jnp.maximum(2 * (ns - 1) - s, s + mb - 1))
+
+    def slot_of(*by_section):
+        at_t = jnp.int32(min(by_section[-1], slots - 1))
+        for sec, value in enumerate(by_section[:-1]):
+            at_t = jnp.where(s == sec, min(value, slots - 1), at_t)
+        return at_t
+
+    t_near = slot_of(4, 5, 0, 0)
+    t_next = slot_of(4, 5, 6, 5)
+    t_last = slot_of(4, 6, 8, 7)
+    t_far = slot_of(7, 8, 9, 8)
+
+    @pl.loop(0, slots)
     def _(t):
         mf = t - s
-        mbk = t - (2 * (ns - 1) - s)
-
-        @pl.when(t == 4 + jnp.where(s == 1, 1, 0))
-        def _():
-            for zeta in range(1, nz):
-                g_z_in(zeta).wait_recv()
-            g_x(x, 0, nz, 0, dev_a).start()
-            g_x(x, 0, nz, 1, dev_b).start()
-            g_d(x, core, 0).start()
-
-        @pl.when(t == 5 + (s + 1) // 2)
-        def _():
-            g_x(na, 0, nz, 0, dev_a).wait_recv()
-            g_x(nb, 0, nz, 1, dev_b).wait_recv()
-            g_x(nb, 0, half, 2, dev_a).start()
-            g_x(na, half, half, 3, dev_b).start()
-            g_d(na, core, 1).start()
-            g_d(nb, core, 2).start()
-
-        @pl.when(t == 2 * (ns - 1) + mb - 1)
-        def _():
-            g_x(opp, 0, half, 2, dev_a).wait_recv()
-            g_x(opp, half, half, 3, dev_b).wait_recv()
-            g_d(opp, core, 3).start()
+        mbk = t - first_b
+
+        @pl.when(jnp.logical_and(t == 0, s > 0))
+        def _():
+            transposed(0)
+
+        @pl.when(t == t_near)
+        def _():
+            from_z(0)
+
+        @pl.when(t == t_next)
+        def _():
+            from_z(1)
+            from_x(0)
+
+        @pl.when(t == t_last)
+        def _():
+            from_x(1)
+
+        @pl.when(t == t_far)
+        def _():
+            from_far()
 
         @pl.when(jnp.logical_and(mf >= 0, mf < mb))
         def _():
@@ -223,7 +274,7 @@
                 slope[mf, :, cols] = hp + hu * (1.0 - bent * bent) * (
                     gelu_coef + (gelu_coef * 3.0 * 0.044715) * uu
                 )
-                acc = acc + dot_nt(hid, w[1, :, cols])
+                acc = acc + dot_nn(hid, wt[1, cols, :])
 
             @pl.when(s < ns - 1)
             def _():
@@ -244,7 +295,7 @@
 
             @pl.when(s > 0)
             def _():
-                bn = dot_nt(right[0, mbk], w[0])
+                bn = dot_nn(right[0, mbk], wt[0])
                 normed = nf[mbk]
                 first = jnp.mean(bn, axis=-1, keepdims=True)
                 second = jnp.mean(bn * normed, axis=-1, keepdims=True)
@@ -256,8 +307,9 @@
     cp_ow.wait()
     cp_var.wait()
     cp_se.wait()
-    for k, xx in enumerate((x, na, nb, opp)):
-        g_d(xx, 1 - core, k).wait_recv()
+    for j, xx in enumerate((x, na, nb, opp)):
+        for k in range(nz):
+            g_d(j, xx, k, 1 - core).wait_recv()
 
     qx = NX // 2
     ct = 512 if hc % 512 == 0 else 256
@@ -297,76 +349,83 @@
 
         @pl.loop(0, nz)
         def _(i):
-            zeta = half + i // 2 - (i % 2) * (1 + 2 * (i // 2))
+            zeta = half + (i % 2) * ((i + 1) // 2 + i // 2) - i // 2
             zz = (z + zeta) % nz
             s0[k, i] = (packed[q, zz, core].astype(F32) + d0[k, zz].astype(F32)).astype(BF)
 
-    def grp(ref, g):
-        return ref.at[pl.ds(g * ng, ng)]
-
     def send_opp(g):
         to = dev_a if g % 2 == 0 else dev_b
-        return remote(grp(s0.at[0], g), grp(ra, g), a_s.at[g], a_r.at[g], to)
+        return remote(s0.at[0, g], ra.at[g], a_s.at[g], a_r.at[g], to)
 
     def send_a(g):
-        return remote(grp(s0.at[1], g), grp(fa, g), ta_s.at[g], ta_r.at[g], dev_a)
+        return remote(s0.at[1, g], fa.at[g], ta_s.at[g], ta_r.at[g], dev_a)
 
     def send_bb(g):
-        return remote(grp(s0.at[2], g), grp(fb, g), tb_s.at[g], tb_r.at[g], dev_b)
-
-    def augment(g):
-        send_opp(g).wait_recv()
-        slot = 2 if g % 2 == 0 else 1
-
-        @pl.loop(0, ng)
-        def _(i):
-            k = g * ng + i
-            s0[slot, k] = (s0[slot, k].astype(F32) + ra[k].astype(F32)).astype(BF)
-
-        (send_bb if slot == 2 else send_a)(g).start()
+        return remote(s0.at[2, g], fb.at[g], tb_s.at[g], tb_r.at[g], dev_b)
+
+    def far(p):
+        send_opp(2 * p).start()
+        send_opp(2 * p + 1).start()
+
+    def near(p):
+        send_a(2 * p).start()
+        send_bb(2 * p + 1).start()
+
+    def augment(p):
+        for g in (2 * p, 2 * p + 1):
+            send_opp(g).wait_recv()
+            slot = 2 if g % 2 == 0 else 1
+            s0[slot, g] = (s0[slot, g].astype(F32) + ra[g].astype(F32)).astype(BF)
+            (send_bb if slot == 2 else send_a)(g).start()
 
     def z_of(k):
-        return half + k // 2 if k % 2 == 0 else half - 1 - k // 2
+        return (half + (k + 1) // 2 if k % 2 else half - k // 2) % nz
 
     def send_z(k):
         return remote(s1.at[k], zr.at[k], z_s.at[k], z_r.at[k], dev_z(z_of(k)))
 
-    def along_z(groups):
-        for g in groups:
-            send_a(g).wait_recv()
-            send_bb(g).wait_recv()
-            for i in range(ng):
-                k = g * ng + i
-                s1[k] = (s0[3, k].astype(F32) + fa[k].astype(F32) + fb[k].astype(F32)).astype(BF)
-                if z_of(k):
-                    send_z(k).start()
-
+    def along_z(p):
+        for k in (2 * p, 2 * p + 1):
+            send_a(k).wait_recv()
+            send_bb(k).wait_recv()
+            s1[k] = (s0[3, k].astype(F32) + fa[k].astype(F32) + fb[k].astype(F32)).astype(BF)
+            if z_of(k):
+                send_z(k).start()
+
+    rounds = nz // 2
     second_pass(opp)
     to_partner(opp, 0).start()
     second_pass(na)
     to_partner(na, 1).start()
     pair_sum(opp, 0)
-    send_opp(0).start()
-    send_opp(1).start()
+    far(0)
     second_pass(nb)
     to_partner(nb, 2).start()
     pair_sum(na, 1)
-    send_a(0).start()
     second_pass(x)
     to_partner(x, 3).start()
     pair_sum(nb, 2)
-    send_bb(1).start()
-    send_opp(2).start()
-    send_opp(3).start()
+    near(0)
+    far(1)
     augment(0)
+    near(1)
+    if rounds > 2:
+        far(2)
+    pair_sum(x, 3)
     augment(1)
-    send_a(2).start()
-    send_bb(3).start()
-    pair_sum(x, 3)
-    augment(2)
-    augment(3)
-    along_z((0, 1))
-    along_z((2, 3))
+    if rounds > 2:
+        near(2)
+        far(3)
+        along_z(0)
+        augment(2)
+        near(3)
+        along_z(1)
+        augment(3)
+        along_z(2)
+        along_z(3)
+    else:
+        along_z(0)
+        along_z(1)
 
     total = s1[nz - 1].astype(F32)
     for k in range(nz - 1):
@@ -391,17 +450,17 @@
         def _():
             send_b(m).wait_send()
 
-    for zeta in range(1, nz):
-        g_z(zeta).wait_send()
-    g_x(x, 0, nz, 0, dev_a).wait_send()
-    g_x(x, 0, nz, 1, dev_b).wait_send()
-    g_x(nb, 0, half, 2, dev_a).wait_send()
-    g_x(na, half, half, 3, dev_b).wait_send()
-    for k, xx in enumerate((x, na, nb, opp)):
-        g_d(xx, core, k).wait_send()
+    for k in range(1, nz):
+        g_z(k).wait_send()
+    for k in range(nz):
+        g_x(x, k, 0).wait_send()
+        g_x(x, k, 1).wait_send()
+        g_y(nb if k % 2 == 0 else na, k).wait_send()
+        for j, xx in enumerate((x, na, nb, opp)):
+            g_d(j, xx, k, core).wait_send()
     for k, q in enumerate((opp, na, nb, x)):
         to_partner(q, k).wait_send()
-    for g in range(4):
+    for g in range(nz):
         send_opp(g).wait_send()
         send_a(g).wait_send()
         send_bb(g).wait_send()
@@ -446,6 +505,7 @@
             pltpu.VMEM((1, 16, hc), BF),
             pltpu.VMEM((1, 16, hc), F32),
             pltpu.VMEM((2, d, hc), BF),
+            pltpu.VMEM((2, hc, d), BF),
             pltpu.VMEM((16, hc), BF),
             pltpu.VMEM(dims, BF),
             pltpu.VMEM(dims, BF),
@@ -468,8 +528,8 @@
             pltpu.VMEM((nz, 16, hc), BF),
             dma((10,)),
             dma((mb,)), dma((mb,)), dma((mb,)), dma((mb,)),
-            dma((nz - 1,)), dma((nz - 1,)), dma((4,)), dma((4,)), dma((4,)), dma((4,)),
-            dma((4,)), dma((4,)), dma((4,)), dma((4,)), dma((4,)), dma((4,)), dma((4,)), dma((4,)),
+            dma((nz,)), dma((nz,)), dma((2, nz)), dma((2, nz)), dma((nz,)), dma((nz,)), dma((4, nz)), dma((4, nz)),
+            dma((4,)), dma((4,)), dma((nz,)), dma((nz,)), dma((nz,)), dma((nz,)), dma((nz,)), dma((nz,)),
             dma((nz,)), dma((nz,)),
         ],
         compiler_params=pltpu.CompilerParams(

time: 89.7 us -> 83.1 us (0.926)
  Pallas kernels: 88.9 us -> 82.4 us
    pallas_call x1, Pallas kernels: 86.8 us -> 80.3 us  [local(): pl.pallas_call(kernel, out_shape=(pltpu.VMEM((1, 16, hc), BF), pltpu.VMEM...]
where the time goes in v3:
time: 83.1 us; the launch traced here: 83 us
  Pallas kernels  82.4 us (99%)
    pallas_call x1, Pallas kernels, local(): pl.pallas_call(kernel, out_shape=(pltpu.VMEM((1, 16, hc), BF), pltpu.VMEM...  80.3 us
    pallas_call x1, Pallas kernels, local(): pl.pallas_call(store_kernel, out_shape=tuple((jax.ShapeDtypeStruct(a.shap...  2.11 us

profile of v3, /device:TPU:1, one launch (start us, length us, event | category | flops | bytes accessed | tf_op | source)
XLA Modules:
  0.0 83.0 jit_solution(5478708463020961892)
XLA Ops:
  0.6 80.3 %step.1 = (bf16[1,16,2048]{2,1,0:T(8,128)(2,1)S(1)}, bf16[1,16,2048]{2,1,0:T(8,128)(2,1)S(1)}, bf16[4,8,2,16,2048]{4,3,2,1,0:T(8,128)(2,1)S(1)}, f32[1,16,2048]{2,1,0:T(8,128)S(1)}) custom-call(s32[4,64]{1,0:T(4,128)} %ids_hbm.1, bf16[128,512]{1,0:T(8,128)(2,1)} %embed_hbm.1, bf16[1,2,512,2048]{3,2,1,0:T(8,128)(2,1)} %w_hbm.1, bf16[1,16,2048]{2,1,0:T(8,128)(2,1)} %var_hbm.1, ...), custom_call_target="tpu_custom_call" | custom-call | tf_op jit(solution)/shard_map/step/pallas_call | solution.py:492
  80.9 2.1 %store.1 = (bf16[1,16,2048]{2,1,0:T(8,128)(2,1)}, bf16[1,16,2048]{2,1,0:T(8,128)(2,1)}, bf16[4,8,2,16,2048]{4,3,2,1,0:T(8,128)(2,1)}, f32[1,16,2048]{2,1,0:T(8,128)}) custom-call(bf16[1,16,2048]{2,1,0:T(8,128)(2,1)S(1)} %get-tuple-element.12.a, bf16[1,16,2048]{2,1,0:T(8,128)(2,1)S(1)} %get-tuple-element.13.b, ...), custom_call_target="tpu_custom_call" | custom-call | tf_op jit(solution)/shard_map/store/pallas_call | solution.py:547

commit v4 on v3

--- a/solution.py
+++ b/solution.py
@@ -92,8 +92,8 @@
         cp_ids.start()
         cp_embed.start()
 
+    cp_w0.start()
     cp_w1.start()
-    cp_w0.start()
     cp_mom.start()
 
     @pl.when(s == ns - 1)
@@ -127,15 +127,9 @@
     def _():
         cp_cot.wait()
 
+    cp_w0.wait()
     cp_w1.wait()
-    transposed(1)
-    cp_w0.wait()
-
-    pl.semaphore_wait(
-        barrier, 2 + nz + jnp.where(s > 0, 1, 0) + jnp.where(s < ns - 1, 1, 0)
-    )
-
-    cp_mom.wait()
+
     order = [0]
     for dist in range(1, half):
         order += [dist, nz - dist]
@@ -164,11 +158,6 @@
     def g_d(j, xx, k, cc):
         blk = mom.at[xx, (z + order[k]) % nz, cc]
         return remote(blk, blk, gd_s.at[j, k], gd_r.at[j, k], partner)
-
-    for k in range(1, nz):
-        g_z(k).start()
-
-    cp_we.start()
 
     def from_z(part):
         for k in parts[part]:
@@ -191,6 +180,14 @@
             g_y(opp, k).wait_recv()
             g_d(3, opp, k, core).start()
 
+    def add_shared(q, j):
+        for k in range(nz):
+            g_d(j, q, k, 1 - core).wait_recv()
+
+        @pl.loop(0, nz)
+        def _(k):
+            comb[q, k] = 0.9 * mom[q, k].astype(F32) + we[q, k].astype(F32)
+
     def send_f(m):
         return pltpu.make_async_remote_copy(
             src_ref=fout.at[m], dst_ref=xin.at[m], send_sem=f_s.at[m], recv_sem=f_r.at[m],
@@ -205,6 +202,35 @@
 
     nt = hc // tile
 
+    def forward(m, second):
+        xv = xin[m].astype(F32)
+        center = jnp.mean(xv, axis=-1, keepdims=True)
+        dev = xv - center
+        spread = jnp.mean(dev * dev, axis=-1, keepdims=True)
+        scaled = lax.rsqrt(spread + 1e-05)
+        normed = dev * scaled
+        nf[m] = normed
+        scf[m] = jnp.broadcast_to(scaled, (tok, 128))
+        nbv = normed.astype(BF)
+        left[0, m] = nbv
+        acc = xv
+        for j in range(nt):
+            cols = slice(j * tile, (j + 1) * tile)
+            u = dot_nn(nbv, w[0, :, cols])
+            uu = u * u
+            bent = jnp.tanh(u * (gelu_coef + (gelu_coef * 0.044715) * uu))
+            hu = 0.5 * u
+            hp = 0.5 + 0.5 * bent
+            hid = (u * hp).astype(BF)
+            right[1, m, :, cols] = hid
+            slope[m, :, cols] = hp + hu * (1.0 - bent * bent) * (
+                gelu_coef + (gelu_coef * 3.0 * 0.044715) * uu
+            )
+            if second is not None:
+                acc = acc + second(hid, cols)
+        if second is not None:
+            fout[m] = acc.astype(BF)
+
     slots = 2 * (ns - 1) + mb
     first_b = jnp.where(s == ns - 1, ns - 1, jnp.maximum(2 * (ns - 1) - s, s + mb - 1))
 
@@ -218,16 +244,35 @@
     t_next = slot_of(4, 5, 6, 5)
     t_last = slot_of(4, 6, 8, 7)
     t_far = slot_of(7, 8, 9, 8)
+    t_shared = slot_of(5, 9, 9, 9)
+
+    @pl.when(s == 0)
+    def _():
+        forward(0, lambda hid, cols: dot_nt(hid, w[1, :, cols]))
+
+    pl.semaphore_wait(
+        barrier, 2 + nz + jnp.where(s > 0, 1, 0) + jnp.where(s < ns - 1, 1, 0)
+    )
+
+    @pl.when(s == 0)
+    def _():
+        send_f(0).start()
+
+    cp_mom.wait()
+    for k in range(1, nz):
+        g_z(k).start()
+    cp_we.start()
+
+    @pl.when(s > 0)
+    def _():
+        transposed(1)
+        transposed(0)
 
     @pl.loop(0, slots)
     def _(t):
         mf = t - s
         mbk = t - first_b
 
-        @pl.when(jnp.logical_and(t == 0, s > 0))
-        def _():
-            transposed(0)
-
         @pl.when(t == t_near)
         def _():
             from_z(0)
@@ -245,41 +290,35 @@
         def _():
             from_far()
 
-        @pl.when(jnp.logical_and(mf >= 0, mf < mb))
-        def _():
-            @pl.when(s > 0)
-            def _():
-                send_f(mf).wait_recv()
-
-            xv = xin[mf].astype(F32)
-            center = jnp.mean(xv, axis=-1, keepdims=True)
-            dev = xv - center
-            spread = jnp.mean(dev * dev, axis=-1, keepdims=True)
-            scaled = lax.rsqrt(spread + 1e-05)
-            normed = dev * scaled
-            nf[mf] = normed
-            scf[mf] = jnp.broadcast_to(scaled, (tok, 128))
-            nbv = normed.astype(BF)
-            left[0, mf] = nbv
-            acc = xv
-            for j in range(nt):
-                cols = slice(j * tile, (j + 1) * tile)
-                u = dot_nn(nbv, w[0, :, cols])
-                uu = u * u
-                bent = jnp.tanh(u * (gelu_coef + (gelu_coef * 0.044715) * uu))
-                hu = 0.5 * u
-                hp = 0.5 + 0.5 * bent
-                hid = (u * hp).astype(BF)
-                right[1, mf, :, cols] = hid
-                slope[mf, :, cols] = hp + hu * (1.0 - bent * bent) * (
-                    gelu_coef + (gelu_coef * 3.0 * 0.044715) * uu
-                )
-                acc = acc + dot_nn(hid, wt[1, cols, :])
-
-            @pl.when(s < ns - 1)
-            def _():
-                fout[mf] = acc.astype(BF)
-                send_f(mf).start()
+        @pl.when(t == t_shared)
+        def _():
+            cp_we.wait()
+            for j, q in enumerate((x, na, nb)):
+                add_shared(q, j)
+
+        @pl.when(t == slots - 1)
+        def _():
+            add_shared(opp, 3)
+
+        has_f = jnp.logical_and(mf >= 0, mf < mb)
+
+        @pl.when(jnp.logical_and(jnp.logical_and(has_f, s == 0), t > 0))
+        def _():
+            forward(mf, lambda hid, cols: dot_nt(hid, w[1, :, cols]))
+
+        @pl.when(jnp.logical_and(has_f, jnp.logical_and(s > 0, s < ns - 1)))
+        def _():
+            send_f(mf).wait_recv()
+            forward(mf, lambda hid, cols: dot_nn(hid, wt[1, cols, :]))
+
+        @pl.when(jnp.logical_and(jnp.logical_and(has_f, s < ns - 1), t > 0))
+        def _():
+            send_f(mf).start()
+
+        @pl.when(jnp.logical_and(has_f, s == ns - 1))
+        def _():
+            send_f(mf).wait_recv()
+            forward(mf, None)
 
         @pl.when(jnp.logical_and(mbk >= 0, mbk < mb))
         def _():
@@ -303,13 +342,9 @@
                 gout[mbk] = (g.astype(F32) + sc * (bn - first - normed * second)).astype(BF)
                 send_b(mbk).start()
 
-    cp_we.wait()
     cp_ow.wait()
     cp_var.wait()
     cp_se.wait()
-    for j, xx in enumerate((x, na, nb, opp)):
-        for k in range(nz):
-            g_d(j, xx, k, 1 - core).wait_recv()
 
     qx = NX // 2
     ct = 512 if hc % 512 == 0 else 256
@@ -322,9 +357,7 @@
         lt = left[i].reshape(mb * tok, d)
         rt = right[i, :, :, pl.ds(j, ct)].reshape(mb * tok, ct)
         grad = dot_tn(lt, rt)
-        shared = mom[pl.ds(i * qx, qx), :, :, :, pl.ds(j, ct)].reshape(rows, ct).astype(F32)
-        err = we[pl.ds(i * qx, qx), :, :, :, pl.ds(j, ct)].reshape(rows, ct).astype(F32)
-        c = 0.9 * shared + 0.1 * grad + err
+        c = comb[pl.ds(i * qx, qx), :, :, :, pl.ds(j, ct)].reshape(rows, ct) + 0.1 * grad
         comb[pl.ds(i * qx, qx), :, :, :, pl.ds(j, ct)] = c.reshape(qx, nz, NC, 16, ct)
         return sq + jnp.sum((c * c).reshape(rows // 8, 8, ct), axis=0)
 
@@ -382,15 +415,20 @@
         return (half + (k + 1) // 2 if k % 2 else half - k // 2) % nz
 
     def send_z(k):
-        return remote(s1.at[k], zr.at[k], z_s.at[k], z_r.at[k], dev_z(z_of(k)))
+        return remote(s1.at[k], zr.at[k], z_s.at[k], z_r.at[k], dev_z(z_of(k) if k else nz - 1))
 
     def along_z(p):
         for k in (2 * p, 2 * p + 1):
             send_a(k).wait_recv()
             send_bb(k).wait_recv()
             s1[k] = (s0[3, k].astype(F32) + fa[k].astype(F32) + fb[k].astype(F32)).astype(BF)
-            if z_of(k):
+            if z_of(k) and k != 1:
                 send_z(k).start()
+
+    def relayed():
+        send_z(0).wait_recv()
+        s1[1] = (s1[1].astype(F32) + zr[0].astype(F32)).astype(BF)
+        send_z(1).start()
 
     rounds = nz // 2
     second_pass(opp)
@@ -420,15 +458,17 @@
         augment(2)
         near(3)
         along_z(1)
+        relayed()
         augment(3)
         along_z(2)
         along_z(3)
     else:
         along_z(0)
+        relayed()
         along_z(1)
 
     total = s1[nz - 1].astype(F32)
-    for k in range(nz - 1):
+    for k in range(1, nz - 1):
         send_z(k).wait_recv()
         total = total + zr[k].astype(F32)
     merged = total * (1.0 / (NX * nz * NC)) + se[0]

time: 83.1 us -> 79.7 us (0.959)
  Pallas kernels: 82.4 us -> 79 us
    pallas_call x1, Pallas kernels: 80.3 us -> 76.9 us  [local(): pl.pallas_call(kernel, out_shape=(pltpu.VMEM((1, 16, hc), BF), pltpu.VMEM...]
where the time goes in v4:
time: 79.7 us; the launch traced here: 79.6 us
  Pallas kernels  79 us (99%)
    pallas_call x1, Pallas kernels, local(): pl.pallas_call(kernel, out_shape=(pltpu.VMEM((1, 16, hc), BF), pltpu.VMEM...  76.9 us
    pallas_call x1, Pallas kernels, local(): pl.pallas_call(store_kernel, out_shape=tuple((jax.ShapeDtypeStruct(a.shap...  2.11 us

profile of v4, /device:TPU:1, one launch (start us, length us, event | category | flops | bytes accessed | tf_op | source)
XLA Modules:
  0.0 79.6 jit_solution(7605595936549186069)
XLA Ops:
  0.6 76.9 %step.1 = (bf16[1,16,2048]{2,1,0:T(8,128)(2,1)S(1)}, bf16[1,16,2048]{2,1,0:T(8,128)(2,1)S(1)}, bf16[4,8,2,16,2048]{4,3,2,1,0:T(8,128)(2,1)S(1)}, f32[1,16,2048]{2,1,0:T(8,128)S(1)}) custom-call(s32[4,64]{1,0:T(4,128)} %ids_hbm.1, bf16[128,512]{1,0:T(8,128)(2,1)} %embed_hbm.1, bf16[1,2,512,2048]{3,2,1,0:T(8,128)(2,1)} %w_hbm.1, bf16[1,16,2048]{2,1,0:T(8,128)(2,1)} %var_hbm.1, ...), custom_call_target="tpu_custom_call" | custom-call | tf_op jit(solution)/shard_map/step/pallas_call | solution.py:532
  77.5 2.1 %store.1 = (bf16[1,16,2048]{2,1,0:T(8,128)(2,1)}, bf16[1,16,2048]{2,1,0:T(8,128)(2,1)}, bf16[4,8,2,16,2048]{4,3,2,1,0:T(8,128)(2,1)}, f32[1,16,2048]{2,1,0:T(8,128)}) custom-call(bf16[1,16,2048]{2,1,0:T(8,128)(2,1)S(1)} %get-tuple-element.12.a, bf16[1,16,2048]{2,1,0:T(8,128)(2,1)S(1)} %get-tuple-element.13.b, ...), custom_call_target="tpu_custom_call" | custom-call | tf_op jit(solution)/shard_map/store/pallas_call | solution.py:587

commit v5 on v4

--- a/solution.py
+++ b/solution.py
@@ -32,7 +32,7 @@
     ns, nz, mb, tok, d, hc, tile,
     ids_hbm, embed_hbm, w_hbm, var_hbm, mom_hbm, we_hbm, se_hbm, cot_hbm,
     nw_ref, nm_ref, ne, nse_ref,
-    ids, embed, var, se, w, wt, own_w, we, mom, comb, packed, xin, fout, gout, nf, scf, slope, left, right,
+    ids, embed, var, se, w, wt, own_w, we, mom, comb, packed, xin, fout, gout, nf, scf, slope, left, right, lt,
     d0, s0, ra, fa, fb, s1, zr,
     loc, f_s, f_r, b_s, b_r, gz_s, gz_r, gx_s, gx_r, gy_s, gy_r, gd_s, gd_r,
     d_s, d_r, a_s, a_r, ta_s, ta_r, tb_s, tb_r, z_s, z_r,
@@ -187,6 +187,9 @@
         @pl.loop(0, nz)
         def _(k):
             comb[q, k] = 0.9 * mom[q, k].astype(F32) + we[q, k].astype(F32)
+
+    def flip(i):
+        lt[i] = left[i].reshape(mb * tok, d).T
 
     def send_f(m):
         return pltpu.make_async_remote_copy(
@@ -295,6 +298,7 @@
             cp_we.wait()
             for j, q in enumerate((x, na, nb)):
                 add_shared(q, j)
+            flip(0)
 
         @pl.when(t == slots - 1)
         def _():
@@ -354,37 +358,58 @@
     def first_pass(idx, sq):
         i = idx // nct
         j = pl.multiple_of((idx % nct) * ct, ct)
-        lt = left[i].reshape(mb * tok, d)
         rt = right[i, :, :, pl.ds(j, ct)].reshape(mb * tok, ct)
-        grad = dot_tn(lt, rt)
+        grad = dot_nn(lt[i], rt)
         c = comb[pl.ds(i * qx, qx), :, :, :, pl.ds(j, ct)].reshape(rows, ct) + 0.1 * grad
         comb[pl.ds(i * qx, qx), :, :, :, pl.ds(j, ct)] = c.reshape(qx, nz, NC, 16, ct)
         return sq + jnp.sum((c * c).reshape(rows // 8, 8, ct), axis=0)
 
+    flip(1)
     sq = lax.fori_loop(0, 2 * nct, first_pass, jnp.zeros((8, ct), F32))
     total_sq = jnp.sum(jnp.sum(sq, axis=0, keepdims=True), axis=1, keepdims=True)
     scale = jnp.sqrt(total_sq * (1.0 / (2 * d * hc)) + 0.01)
     inverse = 1.0 / scale
 
-    def second_pass(q):
-        @pl.loop(0, nz)
+    quarters = (opp, na, nb, x)
+
+    def slot_z(k):
+        zeta = half + (k % 2) * ((k + 1) // 2 + k // 2) - k // 2
+        return (z + zeta) % nz
+
+    def to_partner(j, k):
+        return remote(
+            packed.at[quarters[j], slot_z(k), 1 - core], d0.at[j, k], d_s.at[j, k], d_r.at[j, k], partner
+        )
+
+    def second_pass(j, lo, hi):
+        q = quarters[j]
+
+        @pl.loop(lo, hi)
         def _(k):
-            c = comb[q, k].reshape(NC * 16, hc)
+            zz = slot_z(k)
+            c = comb[q, zz].reshape(NC * 16, hc)
             p = (scale * jnp.tanh(c * inverse)).astype(BF)
-            packed[q, k] = p.reshape(NC, 16, hc)
-            ne[q, k] = (c - p.astype(F32)).astype(BF).reshape(NC, 16, hc)
-
-    def to_partner(q, k):
-        return remote(packed.at[q, pl.ds(0, nz), 1 - core], d0.at[k], d_s.at[k], d_r.at[k], partner)
-
-    def pair_sum(q, k):
-        to_partner(q, k).wait_recv()
-
-        @pl.loop(0, nz)
-        def _(i):
-            zeta = half + (i % 2) * ((i + 1) // 2 + i // 2) - i // 2
-            zz = (z + zeta) % nz
-            s0[k, i] = (packed[q, zz, core].astype(F32) + d0[k, zz].astype(F32)).astype(BF)
+            packed[q, zz] = p.reshape(NC, 16, hc)
+            ne[q, zz] = (c - p.astype(F32)).astype(BF).reshape(NC, 16, hc)
+            to_partner(j, k).start()
+
+    def pair_sum(j, lo, hi):
+        @pl.loop(lo, hi)
+        def _(k):
+            to_partner(j, k).wait_recv()
+            s0[j, k] = (packed[quarters[j], slot_z(k), core].astype(F32) + d0[j, k].astype(F32)).astype(BF)
+
+    def pack(p):
+        for j in range(3):
+            second_pass(j, 2 * p, 2 * p + 2)
+
+    def sum_far(p):
+        pair_sum(0, 2 * p, 2 * p + 2)
+        far(p)
+
+    def sum_near(p):
+        pair_sum(1, 2 * p, 2 * p + 2)
+        pair_sum(2, 2 * p, 2 * p + 2)
 
     def send_opp(g):
         to = dev_a if g % 2 == 0 else dev_b
@@ -431,29 +456,27 @@
         send_z(1).start()
 
     rounds = nz // 2
-    second_pass(opp)
-    to_partner(opp, 0).start()
-    second_pass(na)
-    to_partner(na, 1).start()
-    pair_sum(opp, 0)
-    far(0)
-    second_pass(nb)
-    to_partner(nb, 2).start()
-    pair_sum(na, 1)
-    second_pass(x)
-    to_partner(x, 3).start()
-    pair_sum(nb, 2)
+    pack(0)
+    pack(1)
+    sum_far(0)
+    sum_near(0)
     near(0)
-    far(1)
+    sum_far(1)
+    sum_near(1)
+    for p in range(2, rounds):
+        pack(p)
+    second_pass(3, 0, nz)
     augment(0)
     near(1)
     if rounds > 2:
-        far(2)
-    pair_sum(x, 3)
+        sum_far(2)
+        sum_near(2)
+    pair_sum(3, 0, nz)
     augment(1)
     if rounds > 2:
         near(2)
-        far(3)
+        sum_far(3)
+        sum_near(3)
         along_z(0)
         augment(2)
         near(3)
@@ -498,8 +521,9 @@
         g_y(nb if k % 2 == 0 else na, k).wait_send()
         for j, xx in enumerate((x, na, nb, opp)):
             g_d(j, xx, k, core).wait_send()
-    for k, q in enumerate((opp, na, nb, x)):
-        to_partner(q, k).wait_send()
+    for j in range(4):
+        for k in range(nz):
+            to_partner(j, k).wait_send()
     for g in range(nz):
         send_opp(g).wait_send()
         send_a(g).wait_send()
@@ -527,7 +551,7 @@
     vm = pl.BlockSpec(memory_space=pltpu.VMEM)
     hbm = pl.BlockSpec(memory_space=pl.ANY)
     dma = pltpu.SemaphoreType.DMA
-    tile = 512 if hc % 512 == 0 else 128
+    tile = 1024 if hc % 512 == 0 else 128
     kernel = functools.partial(step_kernel, ns, nz, mb, tok, d, hc, tile)
     nw, nm, ne, nse = pl.pallas_call(
         kernel,
@@ -559,6 +583,7 @@
             pltpu.VMEM((mb, tok, hc), F32),
             pltpu.VMEM((2, mb, tok, d), BF),
             pltpu.VMEM((2, mb, tok, hc), BF),
+            pltpu.VMEM((2, d, mb * tok), BF),
             pltpu.VMEM((4, nz, 16, hc), BF),
             pltpu.VMEM((4, nz, 16, hc), BF),
             pltpu.VMEM((nz, 16, hc), BF),
@@ -569,7 +594,7 @@
             dma((10,)),
             dma((mb,)), dma((mb,)), dma((mb,)), dma((mb,)),
             dma((nz,)), dma((nz,)), dma((2, nz)), dma((2, nz)), dma((nz,)), dma((nz,)), dma((4, nz)), dma((4, nz)),
-            dma((4,)), dma((4,)), dma((nz,)), dma((nz,)), dma((nz,)), dma((nz,)), dma((nz,)), dma((nz,)),
+            dma((4, nz)), dma((4, nz)), dma((nz,)), dma((nz,)), dma((nz,)), dma((nz,)), dma((nz,)), dma((nz,)),
             dma((nz,)), dma((nz,)),
         ],
         compiler_params=pltpu.CompilerParams(

time: 79.7 us -> 77.4 us (0.971)
  Pallas kernels: 79 us -> 76.7 us
    pallas_call x1, Pallas kernels: 76.9 us -> 74.6 us  [local(): pl.pallas_call(kernel, out_shape=(pltpu.VMEM((1, 16, hc), BF), pltpu.VMEM...]
where the time goes in v5:
time: 77.4 us; the launch traced here: 77.3 us
  Pallas kernels  76.7 us (99%)
    pallas_call x1, Pallas kernels, local(): pl.pallas_call(kernel, out_shape=(pltpu.VMEM((1, 16, hc), BF), pltpu.VMEM...  74.6 us
    pallas_call x1, Pallas kernels, local(): pl.pallas_call(store_kernel, out_shape=tuple((jax.ShapeDtypeStruct(a.shap...  2.11 us

profile of v5, /device:TPU:1, one launch (start us, length us, event | category | flops | bytes accessed | tf_op | source)
XLA Modules:
  0.0 77.3 jit_solution(5778677755941049062)
XLA Ops:
  0.6 74.6 %step.1 = (bf16[1,16,2048]{2,1,0:T(8,128)(2,1)S(1)}, bf16[1,16,2048]{2,1,0:T(8,128)(2,1)S(1)}, bf16[4,8,2,16,2048]{4,3,2,1,0:T(8,128)(2,1)S(1)}, f32[1,16,2048]{2,1,0:T(8,128)S(1)}) custom-call(s32[4,64]{1,0:T(4,128)} %ids_hbm.1, bf16[128,512]{1,0:T(8,128)(2,1)} %embed_hbm.1, bf16[1,2,512,2048]{3,2,1,0:T(8,128)(2,1)} %w_hbm.1, bf16[1,16,2048]{2,1,0:T(8,128)(2,1)} %var_hbm.1, ...), custom_call_target="tpu_custom_call" | custom-call | tf_op jit(solution)/shard_map/step/pallas_call | solution.py:556
  75.2 2.1 %store.1 = (bf16[1,16,2048]{2,1,0:T(8,128)(2,1)}, bf16[1,16,2048]{2,1,0:T(8,128)(2,1)}, bf16[4,8,2,16,2048]{4,3,2,1,0:T(8,128)(2,1)}, f32[1,16,2048]{2,1,0:T(8,128)}) custom-call(bf16[1,16,2048]{2,1,0:T(8,128)(2,1)S(1)} %get-tuple-element.12.a, bf16[1,16,2048]{2,1,0:T(8,128)(2,1)S(1)} %get-tuple-element.13.b, ...), custom_call_target="tpu_custom_call" | custom-call | tf_op jit(solution)/shard_map/store/pallas_call | solution.py:612

commit v6 on v5

--- a/solution.py
+++ b/solution.py
@@ -244,9 +244,9 @@
         return at_t
 
     t_near = slot_of(4, 5, 0, 0)
-    t_next = slot_of(4, 5, 6, 5)
-    t_last = slot_of(4, 6, 8, 7)
-    t_far = slot_of(7, 8, 9, 8)
+    t_next = slot_of(4, 5, 6, 6)
+    t_last = slot_of(4, 6, 9, 7)
+    t_far = slot_of(9, 9, 9, 8)
     t_shared = slot_of(5, 9, 9, 9)
 
     @pl.when(s == 0)
@@ -299,10 +299,6 @@
             for j, q in enumerate((x, na, nb)):
                 add_shared(q, j)
             flip(0)
-
-        @pl.when(t == slots - 1)
-        def _():
-            add_shared(opp, 3)
 
         has_f = jnp.logical_and(mf >= 0, mf < mb)
 
@@ -355,9 +351,8 @@
     nct = hc // ct
     rows = qx * nz * NC * 16
 
-    def first_pass(idx, sq):
-        i = idx // nct
-        j = pl.multiple_of((idx % nct) * ct, ct)
+    def first_pass(i, idx, sq):
+        j = pl.multiple_of(idx * ct, ct)
         rt = right[i, :, :, pl.ds(j, ct)].reshape(mb * tok, ct)
         grad = dot_nn(lt[i], rt)
         c = comb[pl.ds(i * qx, qx), :, :, :, pl.ds(j, ct)].reshape(rows, ct) + 0.1 * grad
@@ -365,7 +360,10 @@
         return sq + jnp.sum((c * c).reshape(rows // 8, 8, ct), axis=0)
 
     flip(1)
-    sq = lax.fori_loop(0, 2 * nct, first_pass, jnp.zeros((8, ct), F32))
+    late = opp // 2
+    sq = lax.fori_loop(0, nct, functools.partial(first_pass, 1 - late), jnp.zeros((8, ct), F32))
+    add_shared(opp, 3)
+    sq = lax.fori_loop(0, nct, functools.partial(first_pass, late), sq)
     total_sq = jnp.sum(jnp.sum(sq, axis=0, keepdims=True), axis=1, keepdims=True)
     scale = jnp.sqrt(total_sq * (1.0 / (2 * d * hc)) + 0.01)
     inverse = 1.0 / scale

time: 77.4 us -> 77.9 us (level)
  no operation moved by 1% of the time
where the time goes in v6:
time: 77.9 us; the launch traced here: 77.8 us
  Pallas kernels  77.2 us (99%)
    pallas_call x1, Pallas kernels, local(): pl.pallas_call(kernel, out_shape=(pltpu.VMEM((1, 16, hc), BF), pltpu.VMEM...  75.1 us
    pallas_call x1, Pallas kernels, local(): pl.pallas_call(store_kernel, out_shape=tuple((jax.ShapeDtypeStruct(a.shap...  2.11 us

profile of v6, /device:TPU:1, one launch (start us, length us, event | category | flops | bytes accessed | tf_op | source)
XLA Modules:
  0.0 77.8 jit_solution(17190171333590975945)
XLA Ops:
  0.6 75.1 %step.1 = (bf16[1,16,2048]{2,1,0:T(8,128)(2,1)S(1)}, bf16[1,16,2048]{2,1,0:T(8,128)(2,1)S(1)}, bf16[4,8,2,16,2048]{4,3,2,1,0:T(8,128)(2,1)S(1)}, f32[1,16,2048]{2,1,0:T(8,128)S(1)}) custom-call(s32[4,64]{1,0:T(4,128)} %ids_hbm.1, bf16[128,512]{1,0:T(8,128)(2,1)} %embed_hbm.1, bf16[1,2,512,2048]{3,2,1,0:T(8,128)(2,1)} %w_hbm.1, bf16[1,16,2048]{2,1,0:T(8,128)(2,1)} %var_hbm.1, ...), custom_call_target="tpu_custom_call" | custom-call | tf_op jit(solution)/shard_map/step/pallas_call | solution.py:554
  75.7 2.1 %store.1 = (bf16[1,16,2048]{2,1,0:T(8,128)(2,1)}, bf16[1,16,2048]{2,1,0:T(8,128)(2,1)}, bf16[4,8,2,16,2048]{4,3,2,1,0:T(8,128)(2,1)}, f32[1,16,2048]{2,1,0:T(8,128)}) custom-call(bf16[1,16,2048]{2,1,0:T(8,128)(2,1)S(1)} %get-tuple-element.12.a, bf16[1,16,2048]{2,1,0:T(8,128)(2,1)S(1)} %get-tuple-element.13.b, ...), custom_call_target="tpu_custom_call" | custom-call | tf_op jit(solution)/shard_map/store/pallas_call | solution.py:610

commit v7 on v5

--- a/solution.py
+++ b/solution.py
@@ -351,7 +351,7 @@
     cp_se.wait()
 
     qx = NX // 2
-    ct = 512 if hc % 512 == 0 else 256
+    ct = 1024 if hc % 1024 == 0 else 256
     nct = hc // ct
     rows = qx * nz * NC * 16
 

time: 77.4 us -> 76.8 us (level)
  no operation moved by 1% of the time
where the time goes in v7:
time: 76.8 us; the launch traced here: 76.7 us
  Pallas kernels  76 us (99%)
    pallas_call x1, Pallas kernels, local(): pl.pallas_call(kernel, out_shape=(pltpu.VMEM((1, 16, hc), BF), pltpu.VMEM...  73.9 us
    pallas_call x1, Pallas kernels, local(): pl.pallas_call(store_kernel, out_shape=tuple((jax.ShapeDtypeStruct(a.shap...  2.11 us

profile of v7, /device:TPU:1, one launch (start us, length us, event | category | flops | bytes accessed | tf_op | source)
XLA Modules:
  0.0 76.7 jit_solution(660250884342164073)
XLA Ops:
  0.6 73.9 %step.1 = (bf16[1,16,2048]{2,1,0:T(8,128)(2,1)S(1)}, bf16[1,16,2048]{2,1,0:T(8,128)(2,1)S(1)}, bf16[4,8,2,16,2048]{4,3,2,1,0:T(8,128)(2,1)S(1)}, f32[1,16,2048]{2,1,0:T(8,128)S(1)}) custom-call(s32[4,64]{1,0:T(4,128)} %ids_hbm.1, bf16[128,512]{1,0:T(8,128)(2,1)} %embed_hbm.1, bf16[1,2,512,2048]{3,2,1,0:T(8,128)(2,1)} %w_hbm.1, bf16[1,16,2048]{2,1,0:T(8,128)(2,1)} %var_hbm.1, ...), custom_call_target="tpu_custom_call" | custom-call | tf_op jit(solution)/shard_map/step/pallas_call | solution.py:556
  74.6 2.1 %store.1 = (bf16[1,16,2048]{2,1,0:T(8,128)(2,1)}, bf16[1,16,2048]{2,1,0:T(8,128)(2,1)}, bf16[4,8,2,16,2048]{4,3,2,1,0:T(8,128)(2,1)}, f32[1,16,2048]{2,1,0:T(8,128)}) custom-call(bf16[1,16,2048]{2,1,0:T(8,128)(2,1)S(1)} %get-tuple-element.12.a, bf16[1,16,2048]{2,1,0:T(8,128)(2,1)S(1)} %get-tuple-element.13.b, ...), custom_call_target="tpu_custom_call" | custom-call | tf_op jit(solution)/shard_map/store/pallas_call | solution.py:612
